TPU v7x, 256 devices: a whole 4x4x8 slice. The times are simulated.
256 devices in a mesh: seq: 64 (over y, z, core), tp: 4 (over x).
Axes of the slice: x: 4, y: 4, z: 8, core: 2. Of those that a mesh axis runs over, the one named last changes fastest.
Arguments:
- tokens: bfloat16 [49152, 4096], P('seq'), may hold values from -6 to 6
- query_weight: bfloat16 [4096, 2048], P('seq', 'tp'), may hold values from -0.09375 to 0.09375
- key_weight: bfloat16 [4096, 2048], P('seq', 'tp'), may hold values from -0.09375 to 0.09375
- value_weight: bfloat16 [4096, 2048], P('seq', 'tp'), may hold values from -0.09375 to 0.09375
- gate_weight: bfloat16 [4096, 16], P('seq', 'tp'), may hold values from -0.09375 to 0.09375
- decay_rate: float32 [16], P('tp'), may hold values from 4.0690106e-06 to 0.04
- norm_gain: float32 [2048], P('tp'), may hold values from 0.5 to 1.5
- out_weight: bfloat16 [2048, 4096], P(None, 'tp'), may hold values from -0.125 to 0.125
Outputs:
- mixed: bfloat16 [49152, 4096], P('seq', 'tp')
All inputs are finite; a program needn't handle non-finite values.
Results may differ from a plain program's by a relative error of at most 0.006.
The roundings to bfloat16 on the way count: a program that leaves them out, or rounds other values in their place, can miss the bound.
Values may be sent and summed in bfloat16 or wider, within the bound.
A program may use at most 128 MiB of HBM per device.

v0:
```python
import jax
import jax.numpy as jnp
from jax import lax
from jax.sharding import Mesh
from jax.sharding import PartitionSpec as P

SEQ = ("seq_0", "seq_1", "seq_2")


def side_by_side(arrays, axis, dim, along):
    both = jnp.concatenate(arrays, axis=along)
    whole, at, finished = (lax.all_gather(both, axis, axis=dim, tiled=True), 0, [])
    for a in arrays:
        finished.append(lax.slice_in_dim(whole, at, at + a.shape[along], axis=along))
        at += a.shape[along]
    return tuple(finished)


def nothing_yet(shard, identity):
    return jax.tree.map(
        lambda part, zero: jnp.zeros_like(part) + jnp.asarray(zero, part.dtype), shard, identity
    )


def carried_in(shard, axes, combine, identity):
    before = start = nothing_yet(shard, identity)
    so_far = shard
    for axis in reversed(axes):
        peers, position = (lax.axis_size(axis), lax.axis_index(axis))
        pieces = jax.tree.map(lambda part: lax.all_gather(part, axis), so_far)
        inside, so_far = (start, start)
        for k in range(peers):
            passed = k < position
            so_far = combine(so_far, jax.tree.map(lambda part: part[k], pieces))
            inside = jax.tree.map(lambda new, old: jnp.where(passed, new, old), so_far, inside)
        before = combine(inside, before)
    return before


def on_device(
    tokens, query_weight, key_weight, value_weight, gate_weight, decay_rate, norm_gain, out_weight
):
    tok_rows = tokens.shape[0]
    head_count = decay_rate.shape[0]
    proj_width = query_weight.shape[1]
    head_size = proj_width // head_count

    def contract(piece):
        return jnp.dot(tokens, piece, preferred_element_type=jnp.float32)

    pieces = side_by_side((query_weight, key_weight, value_weight, gate_weight), SEQ, 0, 1)
    query_proj, key_proj, value_proj, gate_logit = tuple(
        (contract(one_piece) for one_piece in pieces)
    )
    query_heads = query_proj.astype(jnp.bfloat16).reshape(tok_rows, head_count, head_size)
    key_heads = key_proj.astype(jnp.bfloat16).reshape(tok_rows, head_count, head_size)
    value_per_head = value_proj.astype(jnp.bfloat16).reshape(tok_rows, head_count, head_size)
    log_decay = -decay_rate[None, :] * jax.nn.softplus(gate_logit)
    within = jnp.cumsum(log_decay, axis=0)
    block_total = within[-1]
    key_scaled = (jnp.exp(block_total[None, :] - within)[:, :, None] * key_heads).astype(
        jnp.bfloat16
    )
    shard_local_state = jnp.einsum(
        "gfw,gfz->fwz", key_scaled, value_per_head, preferred_element_type=jnp.float32
    )

    def decayed_join(earlier, later):
        return (earlier[0] + later[0], jnp.exp(later[0])[:, None, None] * earlier[1] + later[1])

    _, prefix_state = carried_in(
        (block_total, shard_local_state),
        SEQ,
        decayed_join,
        (jnp.zeros_like(block_total), jnp.zeros_like(shard_local_state)),
    )
    query_scaled = (jnp.exp(within)[:, :, None] * query_heads).astype(jnp.bfloat16)
    carried_state = jnp.einsum(
        "fys,ysu->fyu",
        query_scaled,
        prefix_state.astype(jnp.bfloat16),
        preferred_element_type=jnp.float32,
    )
    scores = jnp.einsum("thk,shk->hts", query_heads, key_heads, preferred_element_type=jnp.float32)
    row_index = lax.broadcasted_iota(jnp.int32, (tok_rows, tok_rows), 0)
    col_index = lax.broadcasted_iota(jnp.int32, (tok_rows, tok_rows), 1)
    causal = (col_index <= row_index)[None, :, :]
    decay_gap = within.T[:, :, None] - within.T[:, None, :]
    attn = jnp.where(causal, scores * jnp.exp(jnp.where(causal, decay_gap, 0.0)), 0.0).astype(
        jnp.bfloat16
    )
    local_part = jnp.einsum(
        "hts,shv->thv", attn, value_per_head, preferred_element_type=jnp.float32
    )
    head_out = carried_state + local_part
    mean_square = jnp.mean(head_out * head_out, axis=-1, keepdims=True)
    normed = (head_out * lax.rsqrt(mean_square + 1e-05)).reshape(tok_rows, proj_width) * norm_gain[
        None, :
    ]
    normed = normed.astype(jnp.bfloat16)
    mixed = jnp.dot(
        lax.all_gather(normed, "tp", axis=1, tiled=True),
        out_weight,
        preferred_element_type=jnp.float32,
    )
    return mixed.astype(jnp.bfloat16)


def solution(mesh):
    finer = Mesh(mesh.devices.reshape(4, 8, 2, mesh.shape["tp"]), ("seq_0", "seq_1", "seq_2", "tp"))
    return jax.shard_map(
        on_device,
        mesh=finer,
        in_specs=(
            P(SEQ, None),
            P(SEQ, "tp"),
            P(SEQ, "tp"),
            P(SEQ, "tp"),
            P(SEQ, "tp"),
            P("tp"),
            P("tp"),
            P(None, "tp"),
        ),
        out_specs=P(SEQ, "tp"),
        check_vma=False,
    )
```

profile of v0, /device:TPU:1, one launch (start us, length us, event | category | flops | bytes accessed | tf_op | source)
XLA Modules:
  0.0 258.8 jit_solution(4576178796495780604)
XLA Ops:
  6.5 0.8 copy.26
  7.3 1.6 pad_maximum_fusion
  9.0 0.7 neg.9
  9.7 96.5 %all-gather.9.cloned.1.call-done = bf16[4096,1540]{1,0:T(8,128)(2,1)} async-done(((bf16[64,1540]{1,0:T(8,128)(2,1)}), bf16[4096,1540]{1,0:T(8,128)(2,1)}) %all-gather.9.cloned.1.call-update) | async-done | bytes 12615696 | tf_op jit(solution)/shard_map/all_gather | solution.py:12
  106.2 5.0 %fusion.70 = f32[4,768]{1,0:T(4,128)S(1)} fusion(bf16[768,4096]{1,0:T(8,128)(2,1)} %param.8, bf16[4096,1540]{1,0:T(8,128)(2,1)} %all-gather.9.cloned.1.call-done, f32[4]{0:T(128)S(1)} %neg.9), kind=kOutput, calls=%fused_computation.90 | convolution fusion | flops 25187328 | bytes 7352336 | tf_op jit(solution)/shard_map/dot_general | solution.py:49
  111.2 1.1 reduce-window.6
  112.4 0.2 slice_reduce_fusion
  112.5 0.2 reduce-window.9
  112.7 0.1 add_bitcast_fusion
  112.8 0.2 slice_reduce_fusion.1
  113.0 0.1 subtract_exponential_fusion
  113.1 7.7 %fusion.15 = bf16[512,768]{1,0:T(8,128)(2,1)S(1)} fusion(bf16[768,4096]{1,0:T(8,128)(2,1)} %param.8, bf16[4096,1540]{1,0:T(8,128)(2,1)} %all-gather.9.cloned.1.call-done), kind=kOutput, calls=%fused_computation.21 | convolution fusion | flops 3221618688 | bytes 11272192 | tf_op jit(solution)/shard_map/dot_general | solution.py:49
  120.8 5.9 %fusion.12 = bf16[512,768]{1,0:T(8,128)(2,1)S(1)} fusion(bf16[768,4096]{1,0:T(8,128)(2,1)S(1)} %bitcast.238, bf16[4096,1540]{1,0:T(8,128)(2,1)} %all-gather.9.cloned.1.call-done), kind=kOutput, calls=%fused_computation.20 | convolution fusion | flops 3221618688 | bytes 11272192 | tf_op jit(solution)/shard_map/dot_general | solution.py:49
  126.8 0.4 fusion.23
  127.1 2.2 all-gather
  129.3 1.8 all-gather.1
  131.1 0.8 bitcast_add_fusion.8
  132.0 0.2 iota_compare_fusion
  132.2 11.1 %all-gather.2 = f32[8,1,4]{2,1,0:T(1,128)S(1)} all-gather(f32[1,1,4]{2,1,0:T(1,128)S(1)} %get-tuple-element.23), channel_id=1, replica_groups=mesh['seq_0'=4,'seq_1'=8,'seq_2'=2,'tp'=4] {'seq_1'}, dimensions={0}, use_global_device_ids=true | all-gather | bytes 144 | tf_op jit(solution)/shard_map/all_gather | solution.py:30
  143.4 22.0 %all-gather.11.cloned.1.call-done = f32[8,4,128,128]{3,2,1,0:T(8,128)} async-done(((f32[1,4,128,128]{3,2,1,0:T(8,128)}), f32[8,4,128,128]{3,2,1,0:T(8,128)}) %all-gather.11.cloned.1.call-update) | async-done | bytes 2097168 | tf_op jit(solution)/shard_map/all_gather | solution.py:30
  165.4 2.4 multiply_add_fusion
  167.8 0.2 all-gather.15.cloned.1.call-start
  168.0 7.5 %fusion.18 = bf16[512,768]{1,0:T(8,128)(2,1)S(1)} fusion(bf16[768,4096]{1,0:T(8,128)(2,1)} %param.8, bf16[4096,1540]{1,0:T(8,128)(2,1)} %all-gather.9.cloned.1.call-done), kind=kOutput, calls=%fused_computation.22 | convolution fusion | flops 3221618688 | bytes 11272192 | tf_op jit(solution)/shard_map/dot_general | solution.py:49
  175.6 7.7 %all-gather.3 = f32[4,1,4]{2,1,0:T(1,128)S(1)} all-gather(f32[1,1,4]{2,1,0:T(1,128)S(1)} %get-tuple-element.10), channel_id=1, replica_groups=mesh['seq_0'=4,'seq_1'=8,'seq_2'=2,'tp'=4] {'seq_0'}, dimensions={0}, use_global_device_ids=true | all-gather | bytes 80 | tf_op jit(solution)/shard_map/all_gather | solution.py:30
  183.2 0.4 copy.28
  183.7 6.7 %fusion = f32[4,128,768]{2,1,0:T(8,128)} fusion(bf16[768,4,128]{0,2,1:T(8,128)(2,1)} %bitcast.245, f32[4,768]{1,0:T(4,128)S(1)} %get-tuple-element.9, pred[768,768]{1,0:T(8,128)(4,1)S(1)} %iota_compare_fusion, bf16[768,4,128]{0,2,1:T(8,128)(2,1)S(1)} %bitcast.240, bf16[768,4,128]{0,2,1:T(8,128)(2,1)} %bitcast.247), kind=kOutput, calls=%fused_computation.1 | convolution fusion | flops 1219756032 | bytes 4534272 | tf_op jit(solution)/shard_map/hts,shv->thv/dot_general | solution.py:92
  190.3 5.0 %all-gather.13.cloned.1.call-done = f32[4,4,128,128]{3,2,1,0:T(8,128)} async-done(((f32[1,4,128,128]{3,2,1,0:T(8,128)}), f32[4,4,128,128]{3,2,1,0:T(8,128)}) %all-gather.13.cloned.1.call-update) | async-done | bytes 1048592 | tf_op jit(solution)/shard_map/all_gather | solution.py:30
  195.3 3.5 %fusion.11 = (f32[768,4]{0,1:T(4,128)S(1)}, f32[4,128,768]{2,1,0:T(8,128)S(1)}) fusion(f32[4,128,768]{2,1,0:T(8,128)} %fusion, bf16[768,4,128]{2,0,1:T(8,128)(2,1)S(1)} %copy.28, f32[768,4]{0,1:T(4,128)S(1)} %get-tuple-element.8, f32[4,4,128,128]{3,2,1,0:T(8,128)} %all-gather.13.cloned.1.call-done, f32[8,4,128,128]{3,2,1,0:T(8,128)} %all-gather.11.cloned.1.call-done, ...), kind=kOutput, calls=%fused_computation.16 | convolution fusion | flops 105903104 | bytes 7627022 | tf_op jit(solution)/shard_map/fys,ysu->fyu/dot_general | solution.py:78
  198.9 0.1 bitcast_multiply_fusion.1
  199.0 1.0 fusion.10
  200.1 44.4 %all-gather.15.cloned.1.call-done = bf16[768,2048]{0,1:T(8,128)(2,1)} async-done(((bf16[768,512]{0,1:T(8,128)(2,1)}), bf16[768,2048]{0,1:T(8,128)(2,1)}) %all-gather.15.cloned.1.call-update) | async-done | bytes 3145744 | tf_op jit(solution)/shard_map/all_gather | solution.py:102
  244.5 7.8 %convolution_convert_fusion = bf16[768,1024]{1,0:T(8,128)(2,1)} fusion(bf16[768,2048]{0,1:T(8,128)(2,1)} %all-gather.15.cloned.1.call-done, bf16[2048,1024]{1,0:T(8,128)(2,1)} %param.15), kind=kOutput, calls=%fused_computation.11 | convolution fusion | flops 3222011904 | bytes 8912896 | tf_op jit(solution)/shard_map/dot_general | solution.py:101
  (27 shorter events, 0.3 us)
Async XLA Ops:
  6.5 99.7 %all-gather.9.cloned.1.call-start = ((), (), s32[]{:S(2)}) async-start(), calls=%async_computation | async-start | bytes 13844480 | tf_op jit(solution)/shard_map/all_gather | solution.py:12
  8.9 156.4 %all-gather.11.cloned.1.call-start = ((), (), s32[]{:S(2)}) async-start(), calls=%async_computation.1 | async-start | bytes 2359296 | tf_op jit(solution)/shard_map/all_gather | solution.py:30
  106.2 14.6 %slice-start = ((s8[6291456]{0:T(1024)(128)(4,1)}), s8[2097152]{0:T(1024)(128)(4,1)S(1)}, s32[]{:S(2)}) async-start(s8[6291456]{0:T(1024)(128)(4,1)} %bitcast.237), calls=%async_computation.4 | async-start | bytes 4194304
  113.1 7.7 %slice-start.1 = ((s8[6291456]{0:T(1024)(128)(4,1)}), s8[4194304]{0:T(1024)(128)(4,1)S(1)}, s32[]{:S(2)}) async-start(s8[6291456]{0:T(1024)(128)(4,1)} %bitcast.237), calls=%async_computation.5 | async-start | bytes 8388608
  120.8 6.0 %copy-start.1 = (bf16[512,768]{1,0:T(8,128)(2,1)}, bf16[512,768]{1,0:T(8,128)(2,1)S(1)}, u32[]{:S(2)}) copy-start(bf16[512,768]{1,0:T(8,128)(2,1)S(1)} %fusion.15) | copy-start | bytes 2359300
  126.7 4.4 %copy-start.2 = (bf16[512,768]{1,0:T(8,128)(2,1)}, bf16[512,768]{1,0:T(8,128)(2,1)S(1)}, u32[]{:S(2)}) copy-start(bf16[512,768]{1,0:T(8,128)(2,1)S(1)} %fusion.12) | copy-start | bytes 2359300
  131.9 63.4 %all-gather.13.cloned.1.call-start = ((), (), s32[]{:S(2)}) async-start(), calls=%async_computation.2 | async-start | bytes 1310720 | tf_op jit(solution)/shard_map/all_gather | solution.py:30
  167.8 76.7 %all-gather.15.cloned.1.call-start = ((), (), s32[]{:S(2)}) async-start(), calls=%async_computation.3 | async-start | bytes 3932160 | tf_op jit(solution)/shard_map/all_gather | solution.py:102
  195.3 3.7 %copy-start = (f32[512]{0:T(512)S(1)}, f32[512]{0:T(512)}, u32[]{:S(2)}) copy-start(f32[512]{0:T(512)} %param.14) | copy-start | bytes 6148
Sparse Core Ops, SparseCore 0:
  10.1 96.0 all-gather.8
  132.1 33.2 all-gather.10
  167.9 27.3 all-gather.12
  200.2 44.2 all-gather.14
where the time goes:
time: 259 us
  waiting for transfers between devices  168 us (65%)
  matrix products  44.5 us (17%)
  blocking collectives  22.8 us (9%)
  between operations  13.3 us (5%)
  other arithmetic  8.38 us (3%)
    all_gather x1, waiting for transfers between devices, side_by_side(): lax.all_gather(both, axis, axis=dim, tiled=True)  96.5 us
    all_gather x1, waiting for transfers between devices, on_device(): lax.all_gather(normed, 'tp', axis=1, tiled=True)  44.4 us
    all_gather x2, waiting for transfers between devices, carried_in(): pieces = jax.tree.map(lambda part: lax.all_gather(part, axis), so_far)  27 us
    dot_general x4, matrix products, contract(): return jnp.dot(tokens, piece, preferred_element_type=jnp.float32)  26.1 us
    all_gather x4, blocking collectives, carried_in(): pieces = jax.tree.map(lambda part: lax.all_gather(part, axis), so_far)  22.8 us
    dot_general x1, matrix products, on_device(): jnp.dot(lax.all_gather(normed, 'tp', axis=1, tiled=True), out_weight, pre...  7.75 us
    dot_general x1, matrix products, on_device(): jnp.einsum('hts,shv->thv', attn, value_per_head, preferred_element_type=j...  6.66 us
  transfers between devices with their start and end apart: 4, of which 4 were waited for; matrix products, arithmetic and copies ran while one was open for 6% of the time, Pallas kernels for 0%

commit v1 on v0

v1 whole, which is shorter than its diff:
```python
import functools

import jax
import jax.numpy as jnp
from jax import lax
from jax.experimental import pallas as pl
from jax.experimental.pallas import tpu as pltpu
from jax.sharding import PartitionSpec as P

NY, NZ = 4, 8
MESH = pl.DeviceIdType.MESH
UNITS = (
    ((1, 0), (2, 0)),
    ((1, 1), (2, 1)),
    ((0, 0), (0, 1)),
    ((1, 2), (2, 2)),
    ((1, 3), (2, 3)),
    ((0, 2), (0, 3)),
)
NU = len(UNITS)
A1, A2, B1, B2 = 0, 4, 12, 20


class Ring:
    def __init__(self, item, n, pos, nxt, prv, recv, send, split=True):
        self.item, self.n, self.pos = item, n, pos
        self.nxt, self.prv, self.recv_sem, self.send_sem = nxt, prv, recv, send
        self.split = split

    def legs(self, r):
        last = r == self.n // 2 - 1
        parts = ((None, None), (0, 1))[last and self.split]
        dirs = (0,) if last and not self.split else (0, 1)
        return [(d, parts[d]) for d in dirs]

    def copy(self, idx, part, r, d):
        ref = self.item(lax.rem(idx + 2 * self.n, self.n), part)
        return pltpu.make_async_remote_copy(
            src_ref=ref,
            dst_ref=ref,
            send_sem=self.send_sem,
            recv_sem=self.recv_sem(2 * r + d),
            device_id=(self.nxt, self.prv)[d],
            device_id_type=MESH,
        )

    def send(self, r):
        for d, part in self.legs(r):
            self.copy(self.pos - r if d == 0 else self.pos + r, part, r, d).start()

    def recv(self, r):
        for d, part in self.legs(r):
            self.copy(
                self.pos - 1 - r if d == 0 else self.pos + 1 + r, part, r, d
            ).wait_recv()


def kernel(
    tok_hbm, wq_hbm, wk_hbm, wv_hbm, gate_hbm,
    proj_ref, logit_ref,
    tok, w, gb, gt, load_sem, recv_sem, send_sem, grecv_sem, gsend_sem, pair_send, pair_recv,
):
    s = lax.axis_index("seq")
    y, z, c = s // (2 * NZ), lax.rem(s // 2, NZ), lax.rem(s, 2)

    def seq_id(yy, zz, cc):
        return {"seq": (lax.rem(yy + NY, NY) * NZ + lax.rem(zz + NZ, NZ)) * 2 + cc}

    yp, ym = seq_id(y + 1, z, c), seq_id(y - 1, z, c)
    zp, zm = seq_id(y, z + 1, c), seq_id(y, z - 1, c)
    mate = seq_id(y, z, 1 - c)

    loads = []
    for u, tiles in enumerate(UNITS):
        for t, (m, h) in enumerate(tiles):
            src = (wq_hbm, wk_hbm, wv_hbm)[m].at[:, h * 128 : (h + 1) * 128]
            loads.append(
                pltpu.make_async_copy(src, w.at[u, t, y, z, c], load_sem.at[u * 2 + t])
            )
    loads.append(pltpu.make_async_copy(gate_hbm, gb.at[y, z, c], load_sem.at[2 * NU]))
    for cp in loads:
        cp.start()
    tok_load = pltpu.make_async_copy(tok_hbm, tok, load_sem.at[2 * NU + 1])
    tok_load.start()

    barrier = pltpu.get_barrier_semaphore()
    for dev in (yp, ym, zp, zm, mate):
        pl.semaphore_signal(barrier, inc=1, device_id=dev, device_id_type=MESH)
    pl.semaphore_wait(barrier, 5)
    for cp in loads:
        cp.wait()

    def rows(part):
        return slice(None) if part is None else pl.ds(part * 32, 32)

    def rings(u):
        def make(base, k, item, along_y):
            return Ring(
                item, NY if along_y else NZ, y if along_y else z,
                yp if along_y else zp, ym if along_y else zm,
                lambda i: recv_sem.at[u, base + i], send_sem.at[u, k],
            )

        return (
            make(A1, 0, lambda i, p: w.at[u, 0, i, z, c, rows(p)], True),
            make(A2, 1, lambda i, p: w.at[u, 0, :, i, c, rows(p)], False),
            make(B1, 2, lambda i, p: w.at[u, 1, y, i, c, rows(p)], False),
            make(B2, 3, lambda i, p: w.at[u, 1, i, :, c, rows(p)], True),
        )

    g1 = Ring(lambda i, p: gb.at[i, z, c], NY, y, yp, ym,
              lambda i: grecv_sem.at[i], gsend_sem.at[0], split=False)
    g2 = Ring(lambda i, p: gb.at[:, i, c], NZ, z, zp, zm,
              lambda i: grecv_sem.at[4 + i], gsend_sem.at[1], split=False)

    def to_mate(ring, idx, k):
        ref = ring.item(lax.rem(idx + 2 * ring.n, ring.n), None)
        pltpu.make_async_remote_copy(
            src_ref=ref, dst_ref=ref, send_sem=pair_send.at[k], recv_sem=pair_recv.at[k],
            device_id=mate, device_id_type=MESH,
        ).start()

    def step(j, u):
        a1, a2, b1, b2 = rings(u)
        first = u == 0
        if j == 0:
            @pl.when(first)
            def _():
                g1.send(0)
            a1.send(0)
            b1.send(0)
        elif j == 1:
            @pl.when(first)
            def _():
                g1.recv(0)
                g1.send(1)
            a1.recv(0)
            a1.send(1)
            b1.recv(0)
            b1.send(1)
        elif j == 2:
            @pl.when(first)
            def _():
                g1.recv(1)
                g2.send(0)
                to_mate(g2, z, NU)
            a1.recv(1)
            a2.send(0)
            to_mate(a2, z, u)
            b1.recv(1)
            b1.send(2)
        elif j == 3:
            @pl.when(first)
            def _():
                g2.recv(0)
                g2.send(1)
                to_mate(g2, z + 1, NU)
                to_mate(g2, z - 1, NU)
            b1.recv(2)
            b1.send(3)
            a2.recv(0)
            a2.send(1)
            to_mate(a2, z + 1, u)
            to_mate(a2, z - 1, u)
        elif j == 4:
            @pl.when(first)
            def _():
                g2.recv(1)
                g2.send(2)
                to_mate(g2, z + 2, NU)
                to_mate(g2, z - 2, NU)
            b1.recv(3)
            b2.send(0)
            to_mate(b2, y, u)
            a2.recv(1)
            a2.send(2)
            to_mate(a2, z + 2, u)
            to_mate(a2, z - 2, u)
        elif j == 5:
            @pl.when(first)
            def _():
                g2.recv(2)
                g2.send(3)
                to_mate(g2, z + 3, NU)
                to_mate(g2, z - 3, NU)
            a2.recv(2)
            a2.send(3)
            to_mate(a2, z + 3, u)
            to_mate(a2, z - 3, u)
            b2.recv(0)
            b2.send(1)
            to_mate(b2, y + 1, u)
            to_mate(b2, y - 1, u)
        elif j == 6:
            @pl.when(first)
            def _():
                g2.recv(3)
                to_mate(g2, z + 4, NU)
            a2.recv(3)
            to_mate(a2, z + 4, u)
            b2.recv(1)
            to_mate(b2, y + 2, u)
        else:
            def pair_done(ref, k):
                return pltpu.make_async_remote_copy(
                    src_ref=ref, dst_ref=ref, send_sem=pair_send.at[k],
                    recv_sem=pair_recv.at[k], device_id=mate, device_id_type=MESH,
                )

            def sent(ref, sem):
                pltpu.make_async_remote_copy(
                    src_ref=ref, dst_ref=ref, send_sem=sem, recv_sem=pair_recv.at[0],
                    device_id=mate, device_id_type=MESH,
                ).wait_send()

            @pl.when(first)
            def _():
                pair_done(gb.at[:, :, 1 - c], NU).wait_recv()
                pair_done(gb.at[:, :, c], NU).wait_send()
                sent(gb.at[pl.ds(0, 3), z, c], gsend_sem.at[0])
                sent(gb.at[:, pl.ds(0, 7), c], gsend_sem.at[1])
            pair_done(w.at[u, :, :, :, 1 - c], u).wait_recv()
            pair_done(w.at[u, :, :, :, c], u).wait_send()
            sent(w.at[u, 0, pl.ds(0, 3), z, c], send_sem.at[u, 0])
            sent(w.at[u, 0, :, pl.ds(0, 7), c], send_sem.at[u, 1])
            sent(w.at[u, 1, y, pl.ds(0, 7), c], send_sem.at[u, 2])
            sent(w.at[u, 1, pl.ds(0, 3), :, c], send_sem.at[u, 3])

    def guarded(j, u):
        @pl.when(jnp.logical_and(u >= 0, u < NU))
        def _():
            step(j, u)

    def project(u):
        rhs = jnp.concatenate(
            [w[u, 0].reshape(4096, 128), w[u, 1].reshape(4096, 128)], axis=1
        )

        def chunk(r, _):
            at = pl.ds(pl.multiple_of(r * 256, 256), 256)
            proj_ref[u, at, :] = jnp.dot(
                tok[at, :], rhs, preferred_element_type=jnp.float32
            ).astype(jnp.bfloat16)
            return 0

        lax.fori_loop(0, 3, chunk, 0)

    def gate():
        gt[...] = jnp.zeros_like(gt)
        for yy in range(NY):
            for zz in range(NZ):
                k = (yy * NZ + zz) * 128
                gt[0:16, k : k + 128] = gb[yy, zz, 0] + gb[yy, zz, 1]
        logit_ref[...] = lax.dot_general(
            tok[...], gt[...], (((1,), (1,)), ((), ())), preferred_element_type=jnp.float32
        )

    def slot(i, _):
        for k in range(4):
            guarded(6 - 2 * k, i - 3 + k)
        for k in range(4):
            guarded(7 - 2 * k, i - 3 + k)

        @pl.when(i == 3)
        def _():
            tok_load.wait()
            gate()

        @pl.when(i >= 3)
        def _():
            project(i - 3)

        return 0

    lax.fori_loop(0, NU + 3, slot, 0)


def fused(tokens, wq, wk, wv, gate):
    rows, depth = tokens.shape
    any_spec = pl.BlockSpec(memory_space=pl.ANY)
    vmem = pl.BlockSpec(memory_space=pltpu.VMEM)
    return pl.pallas_call(
        kernel,
        out_shape=(
            jax.ShapeDtypeStruct((NU, rows, 256), jnp.bfloat16),
            jax.ShapeDtypeStruct((rows, 128), jnp.float32),
        ),
        in_specs=[any_spec] * 5,
        out_specs=(vmem, vmem),
        scratch_shapes=[
            pltpu.VMEM((rows, depth), jnp.bfloat16),
            pltpu.VMEM((NU, 2, NY, NZ, 2, 64, 128), jnp.bfloat16),
            pltpu.VMEM((NY, NZ, 2, 16, 128), jnp.bfloat16),
            pltpu.VMEM((128, depth), jnp.bfloat16),
            pltpu.SemaphoreType.DMA((2 * NU + 2,)),
            pltpu.SemaphoreType.DMA((NU, 24)),
            pltpu.SemaphoreType.DMA((NU, 4)),
            pltpu.SemaphoreType.DMA((12,)),
            pltpu.SemaphoreType.DMA((2,)),
            pltpu.SemaphoreType.DMA((NU + 1,)),
            pltpu.SemaphoreType.DMA((NU + 1,)),
        ],
        compiler_params=pltpu.CompilerParams(
            collective_id=0, has_side_effects=True, vmem_limit_bytes=60 * 1024 * 1024
        ),
    )(tokens, wq, wk, wv, gate)


def decayed_join(earlier, later):
    return (earlier[0] + later[0], jnp.exp(later[0])[:, None, None] * earlier[1] + later[1])


def carried_in(total, state):
    s = lax.axis_index("seq")
    totals = lax.all_gather(total, "seq")
    states = lax.all_gather(state, "seq")
    acc = jnp.zeros_like(state)
    for k in range(64):
        acc = jnp.where(k < s, jnp.exp(totals[k])[:, None, None] * acc + states[k], acc)
    return acc


def on_device(tokens, wq, wk, wv, wg, decay_rate, norm_gain, out_weight):
    rows = tokens.shape[0]
    heads, k = 4, 128
    core = lax.rem(lax.axis_index("seq"), 2)
    gt = wg.T
    blank = jnp.zeros_like(gt)
    gate = jnp.concatenate(
        [jnp.where(core == 0, gt, blank), jnp.where(core == 1, gt, blank)], axis=1
    )
    gate = jnp.pad(gate, ((0, 12), (0, 0)))
    proj, logits = fused(tokens, wq, wk, wv, gate)
    slots = {t: (u, i) for u, tiles in enumerate(UNITS) for i, t in enumerate(tiles)}

    def matrix(m):
        parts = [slots[(m, h)] for h in range(heads)]
        return jnp.stack([proj[u, :, i * 128 : (i + 1) * 128] for u, i in parts], axis=1)

    q, kk, v = matrix(0), matrix(1), matrix(2)
    log_decay = -decay_rate[None, :] * jax.nn.softplus(logits[:, :heads])
    within = jnp.cumsum(log_decay, axis=0)
    total = within[-1]
    ks = (jnp.exp(total[None, :] - within)[:, :, None] * kk).astype(jnp.bfloat16)
    local_state = jnp.einsum("gfw,gfz->fwz", ks, v, preferred_element_type=jnp.float32)
    prefix = carried_in(total, local_state)
    qs = (jnp.exp(within)[:, :, None] * q).astype(jnp.bfloat16)
    carried = jnp.einsum(
        "fys,ysu->fyu", qs, prefix.astype(jnp.bfloat16), preferred_element_type=jnp.float32
    )
    scores = jnp.einsum("thk,shk->hts", q, kk, preferred_element_type=jnp.float32)
    causal = jnp.tril(jnp.ones((rows, rows), dtype=bool))[None]
    gap = within.T[:, :, None] - within.T[:, None, :]
    attn = jnp.where(causal, scores * jnp.exp(jnp.where(causal, gap, 0.0)), 0.0).astype(
        jnp.bfloat16
    )
    local = jnp.einsum("hts,shv->thv", attn, v, preferred_element_type=jnp.float32)
    head_out = carried + local
    ms = jnp.mean(head_out * head_out, axis=-1, keepdims=True)
    normed = (head_out * lax.rsqrt(ms + 1e-05)).reshape(rows, heads * k) * norm_gain[None, :]
    normed = normed.astype(jnp.bfloat16)
    mixed = jnp.dot(
        lax.all_gather(normed, "tp", axis=1, tiled=True), out_weight,
        preferred_element_type=jnp.float32,
    )
    return mixed.astype(jnp.bfloat16)


def solution(mesh):
    return jax.shard_map(
        on_device,
        mesh=mesh,
        in_specs=(
            P("seq", None), P("seq", "tp"), P("seq", "tp"), P("seq", "tp"), P("seq", "tp"),
            P("tp"), P("tp"), P(None, "tp"),
        ),
        out_specs=P("seq", "tp"),
        check_vma=False,
    )
```

time: 259 us -> 264 us (1.019)
  Pallas kernels: 0 us -> 89.1 us
  waiting for transfers between devices: 168 us -> 91.8 us
  matrix products: 44.5 us -> 22.9 us
  blocking collectives: 22.8 us -> 37.5 us
    pallas_call x0 -> x1, Pallas kernels: none -> 89.1 us  [fused(): pl.pallas_call(kernel, out_shape=(jax.ShapeDtypeStruct((NU, rows, 256), j...]
    all_gather x3 -> x1, waiting for transfers between devices: 124 us -> 53.2 us  [carried_in(): states = lax.all_gather(state, 'seq')]
    dot_general x7 -> x3, matrix products: 36.7 us -> 15.1 us  [the longest x1 8.27 us: on_device(): jnp.einsum('fys,ysu->fyu', qs, prefix.astype(jnp.bfloat16), preferred_ele...]
    all_gather x4 -> x1, blocking collectives: 22.8 us -> 37.5 us  [carried_in(): totals = lax.all_gather(total, 'seq')]
    all_gather x1, waiting for transfers between devices: 44.4 us -> 38.6 us  [on_device(): lax.all_gather(normed, 'tp', axis=1, tiled=True)]
    add x3 -> x0, other arithmetic: 3.23 us -> none  [the longest x2 3.23 us: decayed_join(): jnp.exp(later[0])[:, None, None] * earlier[1] + later[1]]
  transfers between devices with their start and end apart: 4 -> 2, of which waited for: 4 -> 2; matrix products, arithmetic and copies ran while one was open for 6% -> 2% of each run, Pallas kernels for 0% -> 0%
where the time goes in v1:
time: 264 us
  waiting for transfers between devices  91.8 us (35%)
  Pallas kernels  89.1 us (34%)
  blocking collectives  37.5 us (14%)
  matrix products  22.9 us (9%)
  between operations  13.6 us (5%)
  other arithmetic  6.05 us (2%)
  local copies, waits for them, and re-layouts  3.01 us (1%)
    pallas_call x1, Pallas kernels, fused(): pl.pallas_call(kernel, out_shape=(jax.ShapeDtypeStruct((NU, rows, 256), j...  89.1 us
    all_gather x1, waiting for transfers between devices, carried_in(): states = lax.all_gather(state, 'seq')  53.2 us
    all_gather x1, waiting for transfers between devices, on_device(): lax.all_gather(normed, 'tp', axis=1, tiled=True)  38.6 us
    all_gather x1, blocking collectives, carried_in(): totals = lax.all_gather(total, 'seq')  37.5 us
    dot_general x1, matrix products, on_device(): jnp.einsum('fys,ysu->fyu', qs, prefix.astype(jnp.bfloat16), preferred_ele...  8.27 us
    dot_general x1, matrix products, on_device(): jnp.dot(lax.all_gather(normed, 'tp', axis=1, tiled=True), out_weight, pre...  7.75 us
  transfers between devices with their start and end apart: 2, of which 2 were waited for; matrix products, arithmetic and copies ran while one was open for 2% of the time, Pallas kernels for 0%

profile of v1, /device:TPU:1, one launch (start us, length us, event | category | flops | bytes accessed | tf_op | source)
XLA Modules:
  0.0 264.0 jit_solution(6256546960202592319)
XLA Ops:
  6.5 0.0 all-gather.7.cloned.1.call-start
  6.5 0.7 neg.8
  7.2 0.7 select_bitcast_fusion.1
  7.9 0.7 fusion.78.gate_hbm
  8.5 89.1 %shard_map.82 = (bf16[6,768,256]{2,1,0:T(8,128)(2,1)}, f32[768,128]{1,0:T(8,128)}) custom-call(bf16[768,4096]{1,0:T(8,128)(2,1)} %tok_hbm.1, bf16[64,512]{1,0:T(8,128)(2,1)} %wq_hbm.1, bf16[64,512]{1,0:T(8,128)(2,1)} %wk_hbm.1, bf16[64,512]{1,0:T(8,128)(2,1)} %wv_hbm.1, bf16[16,128]{1,0:T(8,128)(2,1)} %fusion.78.gate_hbm), custom_call_target="tpu_custom_call" | custom-call | tf_op jit(solution)/shard_map/pallas_call | solution.py:282
  97.6 1.2 fusion.9
  98.8 0.2 copy.24
  99.0 1.1 reduce-window.6
  100.2 0.2 slice_reduce_fusion
  100.3 0.2 reduce-window.9
  100.5 0.1 add_bitcast_fusion
  100.6 1.9 slice_bitcast_fusion.11
  102.5 0.2 slice_reduce_fusion.1
  102.6 0.1 subtract_exponential_fusion
  102.7 1.6 fusion.6
  104.3 0.0 all-gather.7.cloned.1.call-update
  104.3 0.0 all-gather.5.cloned.1.call-start
  104.5 37.5 %all-gather.1 = f32[64,1,4]{2,1,0:T(1,128)S(1)} all-gather(f32[1,1,4]{2,1,0:T(1,128)S(1)} %bitcast.183), channel_id=1, replica_groups=mesh['seq'=64,'tp'=4] {'seq'}, dimensions={0}, use_global_device_ids=true | all-gather | bytes 1040 | tf_op jit(solution)/shard_map/all_gather | solution.py:315
  142.0 0.2 iota_compare_fusion
  142.3 5.3 %fusion = f32[4,128,768]{2,1,0:T(8,128)} fusion(f32[4,768]{1,0:T(4,128)S(1)} %get-tuple-element.10, pred[768,768]{1,0:T(8,128)(4,1)S(1)} %iota_compare_fusion, bf16[768,1,128]{2,0,1:T(8,128)(2,1)S(1)} %get-tuple-element.12, bf16[768,1,128]{2,0,1:T(8,128)(2,1)S(1)} %get-tuple-element.13, bf16[768,1,128]{2,0,1:T(8,128)(2,1)S(1)} %get-tuple-element.14, ...), kind=kOutput, calls=%fused_computation.1 | convolution fusion | flops 1223294976 | bytes 4534272 | tf_op jit(solution)/shard_map/hts,shv->thv/dot_general | solution.py:357
  147.6 53.2 %all-gather.7.cloned.1.call-done = f32[256,128,128]{2,1,0:T(8,128)} async-done(((f32[4,128,128]{2,1,0:T(8,128)}), f32[256,128,128]{2,1,0:T(8,128)}) %all-gather.7.cloned.1.call-update) | async-done | bytes 16777232 | tf_op jit(solution)/shard_map/all_gather | solution.py:316
  200.8 8.3 %fusion.5 = (f32[768,4]{0,1:T(4,128)S(1)}, f32[4,128,768]{2,1,0:T(8,128)S(1)}) fusion(f32[4,128,768]{2,1,0:T(8,128)} %fusion, f32[768,4]{0,1:T(4,128)S(1)} %get-tuple-element.9, bf16[768,1,128]{2,0,1:T(8,128)(2,1)S(1)} %get-tuple-element.12, bf16[768,1,128]{2,0,1:T(8,128)(2,1)S(1)} %get-tuple-element.13, bf16[768,1,128]{2,0,1:T(8,128)(2,1)S(1)} %get-tuple-element.14, ...), kind=kOutput, calls=%fused_computation.10 | convolution fusion | flops 116782080 | bytes 20735040 | tf_op jit(solution)/shard_map/fys,ysu->fyu/dot_general | solution.py:348
  209.1 0.0 copy-start
  209.1 0.1 bitcast_multiply_fusion.1
  209.2 0.5 copy-done
  209.7 1.0 fusion.4
  210.8 0.0 all-gather.5.cloned.1.call-update
  210.8 38.6 %all-gather.5.cloned.1.call-done = bf16[768,2048]{0,1:T(8,128)(2,1)} async-done(((bf16[768,512]{0,1:T(8,128)(2,1)}), bf16[768,2048]{0,1:T(8,128)(2,1)}) %all-gather.5.cloned.1.call-update) | async-done | bytes 3145744 | tf_op jit(solution)/shard_map/all_gather | solution.py:363
  249.4 7.8 %convolution_convert_fusion = bf16[768,1024]{1,0:T(8,128)(2,1)} fusion(bf16[768,2048]{0,1:T(8,128)(2,1)} %all-gather.5.cloned.1.call-done, bf16[2048,1024]{1,0:T(8,128)(2,1)} %param.15), kind=kOutput, calls=%fused_computation.5 | convolution fusion | flops 3222011904 | bytes 8912896 | tf_op jit(solution)/shard_map/dot_general | solution.py:362
  (6 shorter events, 0.1 us)
Async XLA Ops:
  6.5 194.2 %all-gather.7.cloned.1.call-start = ((), (), s32[]{:S(2)}) async-start(), calls=%async_computation.1 | async-start | bytes 17039360 | tf_op jit(solution)/shard_map/all_gather | solution.py:316
  104.3 145.0 %all-gather.5.cloned.1.call-start = ((), (), s32[]{:S(2)}) async-start(), calls=%async_computation | async-start | bytes 3932160 | tf_op jit(solution)/shard_map/all_gather | solution.py:363
  209.1 0.7 copy-start
Sparse Core Ops, SparseCore 0:
  104.5 96.2 all-gather.6
  210.9 38.4 all-gather.4

commit v2 on v1

v2 whole, which is shorter than its diff:
```python
import jax
import jax.numpy as jnp
from jax import lax
from jax.experimental import pallas as pl
from jax.experimental.pallas import tpu as pltpu
from jax.sharding import PartitionSpec as P

NX, NY, NZ = 4, 4, 8
MESH = pl.DeviceIdType.MESH
UNITS = (
    ((1, 0), (2, 0)),
    ((1, 1), (2, 1)),
    ((0, 0), (0, 1)),
    ((1, 2), (2, 2)),
    ((1, 3), (2, 3)),
    ((0, 2), (0, 3)),
)
NU = len(UNITS)
NH = 4
A1, A2, B1, B2 = 0, 4, 12, 20


class Ring:
    def __init__(self, item, n, pos, nxt, prv, recv, send, split=True):
        self.item, self.n, self.pos = item, n, pos
        self.nxt, self.prv, self.recv_sem, self.send_sem = nxt, prv, recv, send
        self.split = split

    def legs(self, r):
        last = r == self.n // 2 - 1
        parts = ((None, None), (0, 1))[last and self.split]
        dirs = (0,) if last and not self.split else (0, 1)
        return [(d, parts[d]) for d in dirs]

    def copy(self, idx, part, r, d):
        ref = self.item(lax.rem(idx + 2 * self.n, self.n), part)
        return pltpu.make_async_remote_copy(
            src_ref=ref,
            dst_ref=ref,
            send_sem=self.send_sem,
            recv_sem=self.recv_sem(2 * r + d),
            device_id=(self.nxt, self.prv)[d],
            device_id_type=MESH,
        )

    def send(self, r):
        for d, part in self.legs(r):
            self.copy(self.pos - r if d == 0 else self.pos + r, part, r, d).start()

    def recv(self, r):
        for d, part in self.legs(r):
            self.copy(
                self.pos - 1 - r if d == 0 else self.pos + 1 + r, part, r, d
            ).wait_recv()


def thirds(v):
    hi = v.astype(jnp.bfloat16).astype(jnp.float32)
    mid = (v - hi).astype(jnp.bfloat16).astype(jnp.float32)
    return hi, mid, v - hi - mid


def kernel(
    tok_hbm, wq_hbm, wk_hbm, wv_hbm, gate_hbm, ow_hbm, rate_ref, gain_ref,
    out_ref,
    tok, w, gb, gt, ow, proj, wcol, wrow, total, loc, swap, tz, ty, hand, state, local,
    qs, nb, acc,
    load_sem, recv_sem, send_sem, grecv_sem, gsend_sem, pair_send, pair_recv,
    swap_sem, zs_sem, zr_sem, ys_sem, yr_sem, hand_sem, xs_sem, xr_sem,
):
    x = lax.axis_index("tp")
    s = lax.axis_index("seq")
    y, z, c = s // (2 * NZ), lax.rem(s // 2, NZ), lax.rem(s, 2)

    def seq_id(yy, zz, cc):
        return {"seq": (lax.rem(yy + NY, NY) * NZ + lax.rem(zz + NZ, NZ)) * 2 + cc}

    yp, ym = seq_id(y + 1, z, c), seq_id(y - 1, z, c)
    zp, zm = seq_id(y, z + 1, c), seq_id(y, z - 1, c)
    mate = seq_id(y, z, 1 - c)
    xp, xm = {"tp": lax.rem(x + 1, NX)}, {"tp": lax.rem(x + NX - 1, NX)}

    loads = []
    for u, tiles in enumerate(UNITS):
        for t, (m, h) in enumerate(tiles):
            src = (wq_hbm, wk_hbm, wv_hbm)[m].at[:, h * 128 : (h + 1) * 128]
            loads.append(
                pltpu.make_async_copy(src, w.at[u, t, y, z, c], load_sem.at[u * 2 + t])
            )
    loads.append(pltpu.make_async_copy(gate_hbm, gb.at[y, z, c], load_sem.at[2 * NU]))
    for cp in loads:
        cp.start()
    tok_load = pltpu.make_async_copy(tok_hbm, tok, load_sem.at[2 * NU + 1])
    tok_load.start()
    ow_load = pltpu.make_async_copy(ow_hbm, ow, load_sem.at[2 * NU + 2])
    ow_load.start()

    barrier = pltpu.get_barrier_semaphore()
    for dev in (yp, ym, zp, zm, mate, xp, xm):
        pl.semaphore_signal(barrier, inc=1, device_id=dev, device_id_type=MESH)
    pl.semaphore_wait(barrier, 7)
    for cp in loads:
        cp.wait()

    def rows(part):
        return slice(None) if part is None else pl.ds(part * 32, 32)

    def rings(u):
        def make(base, k, item, along_y):
            return Ring(
                item, NY if along_y else NZ, y if along_y else z,
                yp if along_y else zp, ym if along_y else zm,
                lambda i: recv_sem.at[u, base + i], send_sem.at[u, k],
            )

        return (
            make(A1, 0, lambda i, p: w.at[u, 0, i, z, c, rows(p)], True),
            make(A2, 1, lambda i, p: w.at[u, 0, :, i, c, rows(p)], False),
            make(B1, 2, lambda i, p: w.at[u, 1, y, i, c, rows(p)], False),
            make(B2, 3, lambda i, p: w.at[u, 1, i, :, c, rows(p)], True),
        )

    g1 = Ring(lambda i, p: gb.at[i, z, c], NY, y, yp, ym,
              lambda i: grecv_sem.at[i], gsend_sem.at[0], split=False)
    g2 = Ring(lambda i, p: gb.at[:, i, c], NZ, z, zp, zm,
              lambda i: grecv_sem.at[4 + i], gsend_sem.at[1], split=False)

    def to_mate(ring, idx, k):
        ref = ring.item(lax.rem(idx + 2 * ring.n, ring.n), None)
        pltpu.make_async_remote_copy(
            src_ref=ref, dst_ref=ref, send_sem=pair_send.at[k], recv_sem=pair_recv.at[k],
            device_id=mate, device_id_type=MESH,
        ).start()

    def hop(ring, r):
        if r > 0:
            ring.recv(r - 1)
        if r < ring.n // 2:
            ring.send(r)

    def each(body):
        def one(u, _):
            body(u, rings(u))
            return 0

        lax.fori_loop(0, NU, one, 0)

    def spread():
        g1.send(0)

        def first(u, ring):
            ring[0].send(0)
            ring[2].send(0)

        each(first)
        hop(g1, 1)

        def second(u, ring):
            hop(ring[0], 1)
            hop(ring[2], 1)

        each(second)
        hop(g1, 2)
        g2.send(0)
        to_mate(g2, z, NU)

        def third(u, ring):
            hop(ring[0], 2)
            hop(ring[2], 2)

        each(third)
        a_step(0, 0)
        hop(g2, 1)
        to_mate(g2, z + 1, NU)
        to_mate(g2, z - 1, NU)
        each(lambda u, ring: hop(ring[2], 3))
        a_step(0, 1)
        hop(g2, 2)
        to_mate(g2, z + 2, NU)
        to_mate(g2, z - 2, NU)

        def fifth(u, ring):
            hop(ring[2], 4)

            @pl.when(u == 0)
            def _():
                b_step(0, 0)

        each(fifth)
        a_step(1, 0)
        hop(g2, 3)
        to_mate(g2, z + 3, NU)
        to_mate(g2, z - 3, NU)

    def a_step(r, u):
        ring = rings(u)[1]
        hop(ring, r)
        if r == 0:
            to_mate(ring, z, u)
        elif r < 4:
            to_mate(ring, z + r, u)
            to_mate(ring, z - r, u)
        else:
            to_mate(ring, z + 4, u)

    def b_step(r, u):
        ring = rings(u)[3]
        hop(ring, r)
        if r == 0:
            to_mate(ring, y, u)
        elif r == 1:
            to_mate(ring, y + 1, u)
            to_mate(ring, y - 1, u)
        else:
            to_mate(ring, y + 2, u)

    def valid(fn, u):
        @pl.when(jnp.logical_and(u >= 0, u < NU))
        def _():
            fn(u)

    def tick(t):
        for r in range(4, -1, -1):
            valid(lambda u, r=r: a_step(r, u), t + 2 - r)
            if r < 3:
                valid(lambda u, r=r: b_step(r, u), t + 1 - r)

    def pair_done(ref, k):
        return pltpu.make_async_remote_copy(
            src_ref=ref, dst_ref=ref, send_sem=pair_send.at[k], recv_sem=pair_recv.at[k],
            device_id=mate, device_id_type=MESH,
        )

    def sent(ref, sem):
        pltpu.make_async_remote_copy(
            src_ref=ref, dst_ref=ref, send_sem=sem, recv_sem=pair_recv.at[0],
            device_id=mate, device_id_type=MESH,
        ).wait_send()

    def gate_end():
        hop(g2, 4)
        to_mate(g2, z + 4, NU)
        pair_done(gb.at[:, :, 1 - c], NU).wait_recv()

    def finish():
        pair_done(gb.at[:, :, c], NU).wait_send()
        sent(gb.at[pl.ds(0, 3), z, c], gsend_sem.at[0])
        sent(gb.at[:, pl.ds(0, 7), c], gsend_sem.at[1])

        def one(u, ring):
            pair_done(w.at[u, :, :, :, c], u).wait_send()
            sent(w.at[u, 0, pl.ds(0, 3), z, c], send_sem.at[u, 0])
            sent(w.at[u, 0, :, pl.ds(0, 7), c], send_sem.at[u, 1])
            sent(w.at[u, 1, y, pl.ds(0, 7), c], send_sem.at[u, 2])
            sent(w.at[u, 1, pl.ds(0, 3), :, c], send_sem.at[u, 3])

        each(one)

    def project(u):
        rhs = jnp.concatenate(
            [w[u, 0].reshape(4096, 128), w[u, 1].reshape(4096, 128)], axis=1
        )

        def chunk(r, _):
            at = pl.ds(pl.multiple_of(r * 256, 256), 256)
            proj[u, at, :] = jnp.dot(
                tok[at, :], rhs, preferred_element_type=jnp.float32
            ).astype(jnp.bfloat16)
            return 0

        lax.fori_loop(0, 3, chunk, 0)

    def gate():
        gt[...] = jnp.zeros_like(gt)
        for yy in range(NY):
            for zz in range(NZ):
                k = (yy * NZ + zz) * 128
                gt[0:16, k : k + 128] = gb[yy, zz, 0] + gb[yy, zz, 1]
        logit = lax.dot_general(
            tok[...], gt[...], (((1,), (1,)), ((), ())), preferred_element_type=jnp.float32
        )
        logit = logit.T[0:8, :]
        soft = jnp.maximum(logit, 0.0) + jnp.log1p(jnp.exp(-jnp.abs(logit)))
        decay = -rate_ref[:, 0:1] * soft
        hi, mid, lo = thirds(decay)
        parts = jnp.concatenate([hi, mid, lo, jnp.zeros_like(lo)], axis=0).astype(jnp.bfloat16)
        before = lax.broadcasted_iota(jnp.int32, (768, 768), 0)
        after = lax.broadcasted_iota(jnp.int32, (768, 768), 1)
        upper = jnp.where(before <= after, 1.0, 0.0).astype(jnp.bfloat16)
        sums = jnp.dot(parts, upper, preferred_element_type=jnp.float32)
        within = sums[0:8] + sums[8:16] + sums[16:24]
        column = jnp.concatenate([within, jnp.zeros((120, 768), jnp.float32)], axis=0).T
        for h in range(NH):
            wrow[h] = jnp.broadcast_to(within[h : h + 1, :], (8, 768))
            wcol[h] = jnp.broadcast_to(column[:, h : h + 1], (768, 128))
            total[h] = jnp.broadcast_to(within[h : h + 1, 767:768], (8, 128))

    def half(k):
        return pl.ds(pl.multiple_of(k * 64, 64), 64)

    def local_state(u, h):
        key = proj[u, :, 0:128].astype(jnp.float32)
        scaled = (jnp.exp(total[h, 0:1, :] - wcol[h]) * key).astype(jnp.bfloat16)
        loc[h] = lax.dot_general(
            scaled, proj[u, :, 128:256], (((0,), (0,)), ((), ())),
            preferred_element_type=jnp.float32,
        )
        swap[h, 0, 0:64, :] = loc[h, half(1 - c), :]
        swap[h, 0, 64:72, :] = total[h]
        swap_copy(h).start()

    def swap_copy(h):
        return pltpu.make_async_remote_copy(
            src_ref=swap.at[h, 0], dst_ref=swap.at[h, 1], send_sem=swap_sem.at[h, 0],
            recv_sem=swap_sem.at[h, 1], device_id=mate, device_id_type=MESH,
        )

    def hand_copy(h, k):
        return pltpu.make_async_remote_copy(
            src_ref=hand.at[h], dst_ref=state.at[h, half(k)], send_sem=hand_sem.at[h, 0],
            recv_sem=hand_sem.at[h, 1], device_id=mate, device_id_type=MESH,
        )

    def z_ring(h):
        return Ring(lambda i, p: tz.at[h, i], NZ, z, zp, zm,
                    lambda i: zr_sem.at[h, i], zs_sem.at[h], split=False)

    def y_ring(h):
        return Ring(lambda i, p: ty.at[h, i], NY, y, yp, ym,
                    lambda i: yr_sem.at[h, i], ys_sem.at[h], split=False)

    def x_ring(h):
        def item(i, p):
            return nb.at[h, i] if p is None else nb.at[h, i, pl.ds(p * 384, 384)]

        return Ring(item, NX, x, xp, xm, lambda i: xr_sem.at[h, i], xs_sem.at[h])

    def pack(ref, i, value, log):
        hi, mid, lo = thirds(log)
        row = lax.broadcasted_iota(jnp.int32, (16, 128), 0)
        tail = jnp.where(row == 0, hi, jnp.where(row == 1, mid, jnp.where(row == 2, lo, 0.0)))
        ref[i, 0:64, :] = value.astype(jnp.bfloat16)
        ref[i, 64:80, :] = tail.astype(jnp.bfloat16)

    def unpack(ref, i):
        tail = ref[i, 64:80, :].astype(jnp.float32)
        return ref[i, 0:64, :].astype(jnp.float32), jnp.sum(tail, axis=0, keepdims=True)

    def pair(h):
        mine, theirs = loc[h, half(c), :], swap[h, 1, 0:64, :]
        own, other = total[h, 0:1, :], swap[h, 1, 64:65, :]
        first = c == 0
        return (
            jnp.where(first, mine, theirs), jnp.where(first, own, other),
            jnp.where(first, theirs, mine), jnp.where(first, other, own),
        )

    def below(ref, n, limit):
        acc_s = jnp.zeros((64, 128), jnp.float32)
        acc_a = jnp.zeros((1, 128), jnp.float32)
        kept = (acc_s, acc_a)
        for i in range(n):
            s_i, a_i = unpack(ref, i)
            acc_s, acc_a = jnp.exp(a_i) * acc_s + s_i, acc_a + a_i
            kept = tuple(
                jnp.where(i < limit, new, old) for new, old in zip((acc_s, acc_a), kept)
            )
        return kept, (acc_s, acc_a)

    def scan_step(k, h):
        zr, yr = z_ring(h), y_ring(h)
        if k == 1:
            swap_copy(h).wait_recv()
            s0, a0, s1, a1 = pair(h)
            pack(tz.at[h], z, jnp.exp(a1) * s0 + s1, a0 + a1)
            zr.send(0)
        elif k <= 4:
            hop(zr, k - 1)
        elif k == 5:
            hop(zr, 4)
            _, (row_s, row_a) = below(tz.at[h], NZ, z)
            pack(ty.at[h], y, row_s, row_a)
            yr.send(0)
        elif k == 6:
            hop(yr, 1)
        elif k == 7:
            hop(yr, 2)
            (in_s, in_a), _ = below(tz.at[h], NZ, z)
            (row_s, _), _ = below(ty.at[h], NY, y)
            p0 = jnp.exp(in_a) * row_s + in_s
            s0, a0, _, _ = pair(h)
            p1 = jnp.exp(a0) * p0 + s0
            first = c == 0
            hand[h] = jnp.where(first, p1, p0).astype(jnp.bfloat16)
            hand_copy(h, c).start()
            state[h, half(c), :] = jnp.where(first, p0, p1).astype(jnp.bfloat16)
        else:
            hand_copy(h, 1 - c).wait_recv()

    def attention(u, i, h):
        kv = u - 2 + i
        for r in range(3):
            lo, n = r * 256, (r + 1) * 256
            query = proj[u, lo:n, i * 128 : (i + 1) * 128]
            scores = lax.dot_general(
                query, proj[kv, 0:n, 0:128], (((1,), (1,)), ((), ())),
                preferred_element_type=jnp.float32,
            )
            col = wcol[h, lo:n, :]
            gap = jnp.concatenate([col] * (n // 128), axis=1) - wrow[h, 0:1, 0:n]
            t_at = lax.broadcasted_iota(jnp.int32, (256, n), 0) + lo
            s_at = lax.broadcasted_iota(jnp.int32, (256, n), 1)
            causal = s_at <= t_at
            attn = jnp.where(
                causal, scores * jnp.exp(jnp.where(causal, gap, 0.0)), 0.0
            ).astype(jnp.bfloat16)
            local[h, lo:n, :] = jnp.dot(
                attn, proj[kv, 0:n, 128:256], preferred_element_type=jnp.float32
            )
            qs[h, lo:n, :] = (jnp.exp(col) * query.astype(jnp.float32)).astype(jnp.bfloat16)

    def normed(h):
        out = local[h] + jnp.dot(qs[h], state[h], preferred_element_type=jnp.float32)
        scale = lax.rsqrt(jnp.mean(out * out, axis=-1, keepdims=True) + 1e-05)
        nb[h, x] = (out * scale * gain_ref[h, 0:1, :]).astype(jnp.bfloat16)
        x_ring(h).send(0)

    def mix(h, first, last):
        weight = ow[:, h].reshape(512, 1024)

        def chunk(r, _):
            at = pl.ds(pl.multiple_of(r * 256, 256), 256)
            lhs = jnp.concatenate([nb[h, i, at, :] for i in range(NX)], axis=1)
            part = jnp.dot(lhs, weight, preferred_element_type=jnp.float32)
            if not first:
                part = part + acc[at, :]
            if last:
                out_ref[at, :] = part.astype(jnp.bfloat16)
            else:
                acc[at, :] = part
            return 0

        lax.fori_loop(0, 3, chunk, 0)

    def head_at(u, fn):
        @pl.when((u >= 0) & (u <= 4) & (u != 2))
        def _():
            fn(u - u // 3)

    def point(t, p):
        for k in range(8, 0, -1):
            if (10 + k - p) % 3 == 0:
                head_at(t - (10 + k - p) // 3, lambda h, k=k: scan_step(k, h))

    spread()

    def slot(t, _):
        point(t, 0)
        head_at(t - 6, normed)
        head_at(t - 7, lambda h: hop(x_ring(h), 1))

        @pl.when(t < NU + 3)
        def _():
            tick(t)

        point(t, 1)

        @pl.when(t == 1)
        def _():
            gate_end()
            tok_load.wait()
            gate()

        u = t - 3

        @pl.when((u >= 0) & (u < NU))
        def _():
            pair_done(w.at[u, :, :, :, 1 - c], u).wait_recv()
            project(u)
            head_at(u, lambda h: local_state(u, h))

            @pl.when(lax.rem(u, 3) == 2)
            def _():
                for i in range(2):
                    attention(u, i, (u // 3) * 2 + i)

        point(t, 2)

        def gathered(h):
            hop(x_ring(h), 2)

            @pl.when(h == 0)
            def _():
                ow_load.wait()
                mix(h, True, False)

            @pl.when((h > 0) & (h < NH - 1))
            def _():
                mix(h, False, False)

            @pl.when(h == NH - 1)
            def _():
                mix(h, False, True)

        head_at(t - 8, gathered)
        return 0

    lax.fori_loop(0, 13, slot, 0)
    finish()

    def end(h, _):
        swap_copy(h).wait_send()
        sent(tz.at[h, pl.ds(0, 7)], zs_sem.at[h])
        sent(ty.at[h, pl.ds(0, 3)], ys_sem.at[h])
        hand_copy(h, c).wait_send()
        sent(nb.at[h, pl.ds(0, 3)], xs_sem.at[h])
        return 0

    lax.fori_loop(0, NH, end, 0)


def fused(tokens, wq, wk, wv, gate, ow, rate, gain):
    rows, depth = tokens.shape
    any_spec = pl.BlockSpec(memory_space=pl.ANY)
    vmem = pl.BlockSpec(memory_space=pltpu.VMEM)
    bf16, f32, dma = jnp.bfloat16, jnp.float32, pltpu.SemaphoreType.DMA
    return pl.pallas_call(
        kernel,
        out_shape=jax.ShapeDtypeStruct((rows, ow.shape[-1]), bf16),
        in_specs=[any_spec] * 6 + [vmem] * 2,
        out_specs=vmem,
        scratch_shapes=[
            pltpu.VMEM((rows, depth), bf16),
            pltpu.VMEM((NU, 2, NY, NZ, 2, 64, 128), bf16),
            pltpu.VMEM((NY, NZ, 2, 16, 128), bf16),
            pltpu.VMEM((128, depth), bf16),
            pltpu.VMEM(ow.shape, bf16),
            pltpu.VMEM((NU, rows, 256), bf16),
            pltpu.VMEM((NH, rows, 128), f32),
            pltpu.VMEM((NH, 8, rows), f32),
            pltpu.VMEM((NH, 8, 128), f32),
            pltpu.VMEM((NH, 128, 128), f32),
            pltpu.VMEM((NH, 2, 72, 128), f32),
            pltpu.VMEM((NH, NZ, 80, 128), bf16),
            pltpu.VMEM((NH, NY, 80, 128), bf16),
            pltpu.VMEM((NH, 64, 128), bf16),
            pltpu.VMEM((NH, 128, 128), bf16),
            pltpu.VMEM((NH, rows, 128), f32),
            pltpu.VMEM((NH, rows, 128), bf16),
            pltpu.VMEM((NH, NX, rows, 128), bf16),
            pltpu.VMEM((rows, ow.shape[-1]), f32),
            dma((2 * NU + 3,)), dma((NU, 24)), dma((NU, 4)), dma((12,)), dma((2,)),
            dma((NU + 1,)), dma((NU + 1,)),
            dma((NH, 2)), dma((NH,)), dma((NH, 8)), dma((NH,)), dma((NH, 4)), dma((NH, 2)),
            dma((NH,)), dma((NH, 4)),
        ],
        compiler_params=pltpu.CompilerParams(
            collective_id=0, has_side_effects=True, vmem_limit_bytes=63 * 1024 * 1024
        ),
    )(tokens, wq, wk, wv, gate, ow, rate, gain)


def on_device(tokens, wq, wk, wv, wg, decay_rate, norm_gain, out_weight):
    core = lax.rem(lax.axis_index("seq"), 2)
    gt = wg.T
    blank = jnp.zeros_like(gt)
    gate = jnp.concatenate(
        [jnp.where(core == 0, gt, blank), jnp.where(core == 1, gt, blank)], axis=1
    )
    gate = jnp.pad(gate, ((0, 12), (0, 0)))
    rate = jnp.broadcast_to(jnp.pad(decay_rate, (0, 4))[:, None], (8, 128))
    gain = jnp.broadcast_to(norm_gain.reshape(NH, 1, 128), (NH, 8, 128))
    ow = out_weight.reshape(NX, NH, 128, out_weight.shape[1])
    return fused(tokens, wq, wk, wv, gate, ow, rate, gain)


def solution(mesh):
    return jax.shard_map(
        on_device,
        mesh=mesh,
        in_specs=(
            P("seq", None), P("seq", "tp"), P("seq", "tp"), P("seq", "tp"), P("seq", "tp"),
            P("tp"), P("tp"), P(None, "tp"),
        ),
        out_specs=P("seq", "tp"),
        check_vma=False,
    )
```

time: 264 us -> 138 us (0.52)
  waiting for transfers between devices: 91.8 us -> 0 us
  Pallas kernels: 89.1 us -> 131 us
  blocking collectives: 37.5 us -> 0 us
  matrix products: 22.9 us -> 0 us
  between operations: 13.6 us -> 0.01 us
  other arithmetic: 6.05 us -> 1.36 us
    all_gather x2 -> x0, waiting for transfers between devices: 91.8 us -> none  [the longest x1 53.2 us: carried_in(): states = lax.all_gather(state, 'seq')]
    pallas_call x1, Pallas kernels: 89.1 us -> 131 us  [fused(): pl.pallas_call(kernel, out_shape=jax.ShapeDtypeStruct((rows, ow.shape[-1]...]
    all_gather x1 -> x0, blocking collectives: 37.5 us -> none  [carried_in(): totals = lax.all_gather(total, 'seq')]
    dot_general x4 -> x0, matrix products: 22.9 us -> none  [the longest x1 8.27 us: on_device(): jnp.einsum('fys,ysu->fyu', qs, prefix.astype(jnp.bfloat16), preferred_ele...]
  transfers between devices with their start and end apart: 2 -> 0, of which waited for: 2 -> 0; matrix products, arithmetic and copies ran while one was open for 2% -> 0% of each run, Pallas kernels for 0% -> 0%
where the time goes in v2:
time: 138 us; the launch traced here: 137 us
  Pallas kernels  131 us (95%)
  local copies, waits for them, and re-layouts  5.27 us (4%)
    pallas_call x1, Pallas kernels, fused(): pl.pallas_call(kernel, out_shape=jax.ShapeDtypeStruct((rows, ow.shape[-1]...  131 us

profile of v2, /device:TPU:1, one launch (start us, length us, event | category | flops | bytes accessed | tf_op | source)
XLA Modules:
  0.0 137.3 jit_solution(15618579759963192500)
XLA Ops:
  0.0 0.7 pad.9
  0.7 0.7 select_bitcast_fusion.1
  1.3 0.7 fusion.2.gate_hbm
  2.0 0.7 broadcast_in_dim.17.rate_ref
  2.7 1.3 broadcast_in_dim.19.gain_ref
  4.0 130.7 %shard_map.82 = bf16[768,1024]{1,0:T(8,128)(2,1)} custom-call(bf16[768,4096]{1,0:T(8,128)(2,1)} %tok_hbm.1, bf16[64,512]{1,0:T(8,128)(2,1)} %wq_hbm.1, bf16[64,512]{1,0:T(8,128)(2,1)} %wk_hbm.1, bf16[64,512]{1,0:T(8,128)(2,1)} %wv_hbm.1, bf16[16,128]{1,0:T(8,128)(2,1)} %fusion.2.gate_hbm, bf16[4,4,128,1024]{3,2,1,0:T(8,128)(2,1)} %bitcast.6, ...), custom_call_target="tpu_custom_call" | custom-call | tf_op jit(solution)/shard_map/pallas_call | solution.py:527
  134.6 2.7 %copy.10 = bf16[768,1024]{1,0:T(8,128)(2,1)} copy(bf16[768,1024]{1,0:T(8,128)(2,1)} %shard_map.82) | data formatting | bytes 3145728

commit v3 on v2

v3 whole, which is shorter than its diff:
```python
import jax
import jax.numpy as jnp
from jax import lax
from jax.experimental import pallas as pl
from jax.experimental.pallas import tpu as pltpu
from jax.sharding import PartitionSpec as P

NX, NY, NZ = 4, 4, 8
MESH = pl.DeviceIdType.MESH
UNITS = (
    ((1, 0), (2, 0)),
    ((1, 1), (2, 1)),
    ((1, 2), (2, 2)),
    ((1, 3), (2, 3)),
    ((0, 0), (0, 1)),
    ((0, 2), (0, 3)),
)
NU = len(UNITS)
NH = 4
NB = NU // 2
A1, A2, B1, B2 = 0, 4, 12, 20


class Ring:
    def __init__(self, item, n, pos, nxt, prv, recv, send, split=True):
        self.item, self.n, self.pos = item, n, pos
        self.nxt, self.prv, self.recv_sem, self.send_sem = nxt, prv, recv, send
        self.split = split

    def legs(self, r):
        last = r == self.n // 2 - 1
        parts = ((None, None), (0, 1))[last and self.split]
        dirs = (0,) if last and not self.split else (0, 1)
        return [(d, parts[d]) for d in dirs]

    def copy(self, idx, part, r, d):
        ref = self.item(lax.rem(idx + 2 * self.n, self.n), part)
        return pltpu.make_async_remote_copy(
            src_ref=ref,
            dst_ref=ref,
            send_sem=self.send_sem,
            recv_sem=self.recv_sem(2 * r + d),
            device_id=(self.nxt, self.prv)[d],
            device_id_type=MESH,
        )

    def send(self, r):
        for d, part in self.legs(r):
            self.copy(self.pos - r if d == 0 else self.pos + r, part, r, d).start()

    def recv(self, r):
        for d, part in self.legs(r):
            self.copy(
                self.pos - 1 - r if d == 0 else self.pos + 1 + r, part, r, d
            ).wait_recv()


def thirds(v):
    hi = v.astype(jnp.bfloat16).astype(jnp.float32)
    mid = (v - hi).astype(jnp.bfloat16).astype(jnp.float32)
    return hi, mid, v - hi - mid


def kernel(
    tok_hbm, wq_hbm, wk_hbm, wv_hbm, ow_hbm, gate_ref, rate_ref, gain_ref,
    out_ref,
    tok, w, gb, gt, ow, proj, wcol, wrow, total, loc, swap, tz, ty, hand, state, local,
    qs, nb, acc,
    load_sem, recv_sem, send_sem, grecv_sem, gsend_sem, pair_send, pair_recv,
    swap_sem, zs_sem, zr_sem, ys_sem, yr_sem, hand_sem, xs_sem, xr_sem,
):
    x = lax.axis_index("tp")
    s = lax.axis_index("seq")
    y, z, c = s // (2 * NZ), lax.rem(s // 2, NZ), lax.rem(s, 2)

    def seq_id(yy, zz, cc):
        return {"seq": (lax.rem(yy + NY, NY) * NZ + lax.rem(zz + NZ, NZ)) * 2 + cc}

    yp, ym = seq_id(y + 1, z, c), seq_id(y - 1, z, c)
    zp, zm = seq_id(y, z + 1, c), seq_id(y, z - 1, c)
    mate = seq_id(y, z, 1 - c)
    xp, xm = {"tp": lax.rem(x + 1, NX)}, {"tp": lax.rem(x + NX - 1, NX)}

    loads = []
    for u, tiles in enumerate(UNITS):
        for t, (m, h) in enumerate(tiles):
            src = (wq_hbm, wk_hbm, wv_hbm)[m].at[:, h * 128 : (h + 1) * 128]
            loads.append(
                pltpu.make_async_copy(src, w.at[u, t, y, z, c], load_sem.at[u * 2 + t])
            )
    for cp in loads:
        cp.start()
    tok_load = pltpu.make_async_copy(tok_hbm, tok, load_sem.at[2 * NU + 1])
    tok_load.start()
    ow_load = pltpu.make_async_copy(ow_hbm, ow, load_sem.at[2 * NU + 2])
    ow_load.start()

    barrier = pltpu.get_barrier_semaphore()
    partners = [seq_id(y, z + d, c) for d in range(1, NZ)]
    partners += [seq_id(y + d, z, c) for d in range(1, NY)]
    partners += [mate, xp, xm]
    for dev in partners:
        pl.semaphore_signal(barrier, inc=1, device_id=dev, device_id_type=MESH)
    pl.semaphore_wait(barrier, len(partners))

    def rows(part):
        return slice(None) if part is None else pl.ds(part * 32, 32)

    def piece(b, tile, yy, zz, part):
        return w.at[pl.ds(2 * b, 2), tile, lax.rem(yy + NY, NY), lax.rem(zz + NZ, NZ), c, rows(part)]

    def rings(b):
        made = []

        def make(item, along_y, wait):
            count = len(made)
            base = (0, 4, 12, 20, 28, 36)[count] if count < 6 else 44 + 4 * (count - 6)
            made.append((wait, Ring(
                item, NY if along_y else NZ, y if along_y else z,
                yp if along_y else zp, ym if along_y else zm,
                lambda i: recv_sem.at[b, base + i], send_sem.at[b, count if count < 2 else 2 if count < 6 else 3],
            )))

        make(lambda i, p: piece(b, 0, i, z, p), True, 0)
        make(lambda i, p: piece(b, 1, y, i, p), False, 0)
        for d in (0, 1, -1, 2):
            make(lambda i, p, d=d: piece(b, 0, y + d, i, p), False, abs(d))
        for d in (0, 1, -1, 2, -2, 3, -3, 4):
            make(lambda i, p, d=d: piece(b, 1, i, z + d, p), True, abs(d))
        return made

    g1 = Ring(lambda i, p: gb.at[i, z, c], NY, y, yp, ym,
              lambda i: grecv_sem.at[i], gsend_sem.at[0], split=False)
    g2 = Ring(lambda i, p: gb.at[:, i, c], NZ, z, zp, zm,
              lambda i: grecv_sem.at[4 + i], gsend_sem.at[1], split=False)

    def to_mate(ring, idx, k):
        ref = ring.item(lax.rem(idx + 2 * ring.n, ring.n), None)
        pltpu.make_async_remote_copy(
            src_ref=ref, dst_ref=ref, send_sem=pair_send.at[k], recv_sem=pair_recv.at[k],
            device_id=mate, device_id_type=MESH,
        ).start()

    def hop(ring, r):
        if r > 0:
            ring.recv(r - 1)
        if r < ring.n // 2:
            ring.send(r)

    def load_gate():
        k = lax.broadcasted_iota(jnp.int32, (64, 128), 0)
        lane = lax.broadcasted_iota(jnp.int32, (64, 128), 1)
        pick = jnp.where(lane == k + 64 * c, 1.0, 0.0).astype(jnp.bfloat16)
        turned = lax.dot_general(
            gate_ref[...], pick, (((0,), (0,)), ((), ())), preferred_element_type=jnp.float32
        )
        gb[y, z, c] = jnp.concatenate(
            [turned, jnp.zeros((12, 128), jnp.float32)], axis=0
        ).astype(jnp.bfloat16)

    def column(b, zz):
        ref = w.at[pl.ds(2 * b, 2), :, :, lax.rem(zz + NZ, NZ), c]
        pltpu.make_async_remote_copy(
            src_ref=ref, dst_ref=ref, send_sem=pair_send.at[b], recv_sem=pair_recv.at[b],
            device_id=mate, device_id_type=MESH,
        ).start()

    def gate_round(k):
        if k <= 2:
            hop(g1, k)
        if k >= 2:
            hop(g2, k - 2)
            d = k - 2
            for at in {0: (z,), 4: (z + 4,)}.get(d, (z + d, z - d)):
                to_mate(g2, at, NB)

    def weight_round(k, b):
        if k == 0:
            for i in range(2):
                for t in range(2):
                    own = w.at[2 * b + i, t, y, z, c]
                    pltpu.make_async_copy(own, own, load_sem.at[b * 4 + 2 * i + t]).wait()

            @pl.when(b == 0)
            def _():
                load_gate()

        @pl.when(b == 0)
        def _():
            gate_round(k)

        todo = [(ring, k - wait) for wait, ring in rings(b)]
        for ring, r in todo:
            if 0 < r <= ring.n // 2:
                ring.recv(r - 1)
            if 0 <= r < ring.n // 2:
                ring.send(r)
        if k >= 2:
            d = k - 2
            for at in {0: (z,), 4: (z + 4,)}.get(d, (z + d, z - d)):
                column(b, at)

    def valid(k, b):
        @pl.when((b >= 0) & (b < NB))
        def _():
            weight_round(k, b)

    def pair_done(ref, k):
        return pltpu.make_async_remote_copy(
            src_ref=ref, dst_ref=ref, send_sem=pair_send.at[k], recv_sem=pair_recv.at[k],
            device_id=mate, device_id_type=MESH,
        )

    def sent(ref, sem):
        pltpu.make_async_remote_copy(
            src_ref=ref, dst_ref=ref, send_sem=sem, recv_sem=pair_recv.at[0],
            device_id=mate, device_id_type=MESH,
        ).wait_send()

    def finish():
        pair_done(gb.at[:, :, c], NB).wait_send()
        sent(gb.at[pl.ds(0, 3), z, c], gsend_sem.at[0])
        sent(gb.at[:, pl.ds(0, 7), c], gsend_sem.at[1])

        def one(b, _):
            two = pl.ds(2 * b, 2)
            pair_done(w.at[two, :, :, :, c], b).wait_send()
            sent(w.at[two, 0, pl.ds(0, 3), z, c], send_sem.at[b, 0])
            sent(w.at[two, 1, y, pl.ds(0, 7), c], send_sem.at[b, 1])
            sent(w.at[two, 0, :, pl.ds(0, 7), c], send_sem.at[b, 2])
            sent(w.at[two, 1, pl.ds(0, 3), :, c], send_sem.at[b, 3])
            return 0

        lax.fori_loop(0, NB, one, 0)

    def project(u):
        rhs = jnp.concatenate(
            [w[u, 0].reshape(4096, 128), w[u, 1].reshape(4096, 128)], axis=1
        )

        def chunk(r, _):
            at = pl.ds(pl.multiple_of(r * 256, 256), 256)
            proj[u, at, :] = jnp.dot(
                tok[at, :], rhs, preferred_element_type=jnp.float32
            ).astype(jnp.bfloat16)
            return 0

        lax.fori_loop(0, 3, chunk, 0)

    def gate():
        gt[...] = jnp.zeros_like(gt)
        for yy in range(NY):
            for zz in range(NZ):
                k = (yy * NZ + zz) * 128
                gt[0:16, k : k + 128] = gb[yy, zz, 0] + gb[yy, zz, 1]
        logit = lax.dot_general(
            tok[...], gt[...], (((1,), (1,)), ((), ())), preferred_element_type=jnp.float32
        )
        logit = logit.T[0:8, :]
        soft = jnp.maximum(logit, 0.0) + jnp.log1p(jnp.exp(-jnp.abs(logit)))
        head = lax.broadcasted_iota(jnp.int32, (8, 128), 0)
        rate = jnp.zeros((8, 128), jnp.float32)
        for h in range(NH):
            rate = jnp.where(head == h, rate_ref[h], rate)
        decay = -rate[:, 0:1] * soft
        hi, mid, lo = thirds(decay)
        parts = jnp.concatenate([hi, mid, lo, jnp.zeros_like(lo)], axis=0).astype(jnp.bfloat16)
        before = lax.broadcasted_iota(jnp.int32, (768, 768), 0)
        after = lax.broadcasted_iota(jnp.int32, (768, 768), 1)
        upper = jnp.where(before <= after, 1.0, 0.0).astype(jnp.bfloat16)
        sums = jnp.dot(parts, upper, preferred_element_type=jnp.float32)
        within = sums[0:8] + sums[8:16] + sums[16:24]
        column = jnp.concatenate([within, jnp.zeros((120, 768), jnp.float32)], axis=0).T
        for h in range(NH):
            wrow[h] = jnp.broadcast_to(within[h : h + 1, :], (8, 768))
            wcol[h] = jnp.broadcast_to(column[:, h : h + 1], (768, 128))
            total[h] = jnp.broadcast_to(within[h : h + 1, 767:768], (8, 128))

    def half(k):
        return pl.ds(pl.multiple_of(k * 64, 64), 64)

    def local_state(u, h):
        key = proj[u, :, 0:128].astype(jnp.float32)
        scaled = (jnp.exp(total[h, 0:1, :] - wcol[h]) * key).astype(jnp.bfloat16)
        loc[h] = lax.dot_general(
            scaled, proj[u, :, 128:256], (((0,), (0,)), ((), ())),
            preferred_element_type=jnp.float32,
        )
        q, i = h // 2, lax.rem(h, 2)
        swap[q, 0, i, 0:64, :] = loc[h, half(1 - c), :]
        swap[q, 0, i, 64:72, :] = total[h]

    def swap_copy(q):
        return pltpu.make_async_remote_copy(
            src_ref=swap.at[q, 0], dst_ref=swap.at[q, 1], send_sem=swap_sem.at[q, 0],
            recv_sem=swap_sem.at[q, 1], device_id=mate, device_id_type=MESH,
        )

    def hand_copy(q, k):
        return pltpu.make_async_remote_copy(
            src_ref=hand.at[q], dst_ref=state.at[pl.ds(2 * q, 2), half(k)],
            send_sem=hand_sem.at[q, 0], recv_sem=hand_sem.at[q, 1],
            device_id=mate, device_id_type=MESH,
        )

    def all_z(q, d, src):
        ref = tz.at[q, lax.rem(src + NZ, NZ)]
        return pltpu.make_async_remote_copy(
            src_ref=ref, dst_ref=ref, send_sem=zs_sem.at[q], recv_sem=zr_sem.at[q, d - 1],
            device_id=seq_id(y, z + d, c), device_id_type=MESH,
        )

    def all_y(q, d, src):
        ref = ty.at[q, lax.rem(src + NY, NY)]
        return pltpu.make_async_remote_copy(
            src_ref=ref, dst_ref=ref, send_sem=ys_sem.at[q], recv_sem=yr_sem.at[q, d - 1],
            device_id=seq_id(y + d, z, c), device_id_type=MESH,
        )

    def x_ring(h):
        def item(i, p):
            return nb.at[h, i] if p is None else nb.at[h, i, pl.ds(p * 384, 384)]

        return Ring(item, NX, x, xp, xm, lambda i: xr_sem.at[h, i], xs_sem.at[h])

    def pack(ref, at, i, value, log):
        hi, mid, lo = thirds(log)
        row = lax.broadcasted_iota(jnp.int32, (16, 128), 0)
        tail = jnp.where(row == 0, hi, jnp.where(row == 1, mid, jnp.where(row == 2, lo, 0.0)))
        ref[at, i, 0:64, :] = value.astype(jnp.bfloat16)
        ref[at, i, 64:80, :] = tail.astype(jnp.bfloat16)

    def unpack(ref, at, i):
        tail = ref[at, i, 64:80, :].astype(jnp.float32)
        return ref[at, i, 0:64, :].astype(jnp.float32), jnp.sum(tail, axis=0, keepdims=True)

    def pair(q, i):
        h = 2 * q + i
        mine, theirs = loc[h, half(c), :], swap[q, 1, i, 0:64, :]
        own, other = total[h, 0:1, :], swap[q, 1, i, 64:65, :]
        first = c == 0
        return (
            jnp.where(first, mine, theirs), jnp.where(first, own, other),
            jnp.where(first, theirs, mine), jnp.where(first, other, own),
        )

    def below(ref, i, n, limit):
        acc_s = jnp.zeros((64, 128), jnp.float32)
        acc_a = jnp.zeros((1, 128), jnp.float32)
        kept = (acc_s, acc_a)
        for at in range(n):
            s_at, a_at = unpack(ref, at, i)
            acc_s, acc_a = jnp.exp(a_at) * acc_s + s_at, acc_a + a_at
            kept = tuple(
                jnp.where(at < limit, new, old) for new, old in zip((acc_s, acc_a), kept)
            )
        return kept, (acc_s, acc_a)

    def scan_step(k, q):
        if k == 1:
            swap_copy(q).wait_recv()
            for i in range(2):
                s0, a0, s1, a1 = pair(q, i)
                pack(tz.at[q], z, i, jnp.exp(a1) * s0 + s1, a0 + a1)
            for d in (4, 3, 5, 2, 6, 1, 7):
                all_z(q, d, z).start()
        elif k == 2:
            for d in range(1, NZ):
                all_z(q, d, z - d).wait_recv()
            for i in range(2):
                _, (row_s, row_a) = below(tz.at[q], i, NZ, z)
                pack(ty.at[q], y, i, row_s, row_a)
            for d in (2, 1, 3):
                all_y(q, d, y).start()
        elif k == 3:
            for d in range(1, NY):
                all_y(q, d, y - d).wait_recv()
            first = c == 0
            for i in range(2):
                (in_s, in_a), _ = below(tz.at[q], i, NZ, z)
                (row_s, _), _ = below(ty.at[q], i, NY, y)
                p0 = jnp.exp(in_a) * row_s + in_s
                s0, a0, _, _ = pair(q, i)
                p1 = jnp.exp(a0) * p0 + s0
                hand[q, i] = jnp.where(first, p1, p0).astype(jnp.bfloat16)
                state[2 * q + i, half(c), :] = jnp.where(first, p0, p1).astype(jnp.bfloat16)
            hand_copy(q, c).start()
        else:
            hand_copy(q, 1 - c).wait_recv()

    def attention(u, i, h):
        kv = h
        for r in range(3):
            lo, n = r * 256, (r + 1) * 256
            query = proj[u, lo:n, i * 128 : (i + 1) * 128]
            scores = lax.dot_general(
                query, proj[kv, 0:n, 0:128], (((1,), (1,)), ((), ())),
                preferred_element_type=jnp.float32,
            )
            col = wcol[h, lo:n, :]
            gap = jnp.concatenate([col] * (n // 128), axis=1) - wrow[h, 0:1, 0:n]
            t_at = lax.broadcasted_iota(jnp.int32, (256, n), 0) + lo
            s_at = lax.broadcasted_iota(jnp.int32, (256, n), 1)
            causal = s_at <= t_at
            attn = jnp.where(
                causal, scores * jnp.exp(jnp.where(causal, gap, 0.0)), 0.0
            ).astype(jnp.bfloat16)
            local[h, lo:n, :] = jnp.dot(
                attn, proj[kv, 0:n, 128:256], preferred_element_type=jnp.float32
            )
            qs[h, lo:n, :] = (jnp.exp(col) * query.astype(jnp.float32)).astype(jnp.bfloat16)

    def normed(h):
        out = local[h] + jnp.dot(qs[h], state[h], preferred_element_type=jnp.float32)
        scale = lax.rsqrt(jnp.mean(out * out, axis=-1, keepdims=True) + 1e-05)
        nb[h, x] = (out * scale * gain_ref[pl.ds(h, 1), :]).astype(jnp.bfloat16)
        x_ring(h).send(0)

    def mix(h, first, last):
        weight = ow[:, h].reshape(512, 1024)

        def chunk(r, _):
            at = pl.ds(pl.multiple_of(r * 256, 256), 256)
            lhs = jnp.concatenate([nb[h, i, at, :] for i in range(NX)], axis=1)
            part = jnp.dot(lhs, weight, preferred_element_type=jnp.float32)
            if not first:
                part = part + acc[at, :]
            if last:
                out_ref[at, :] = part.astype(jnp.bfloat16)
            else:
                acc[at, :] = part
            return 0

        lax.fori_loop(0, 3, chunk, 0)

    def slot(i, _):
        b = i - 3
        for k in (6, 4, 2, 0):
            valid(k, i - k // 2)

        @pl.when(i == 3)
        def _():
            pair_done(gb.at[:, :, 1 - c], NB).wait_recv()
            tok_load.wait()
            gate()

        @pl.when(i == 4)
        def _():
            scan_step(1, 0)

        @pl.when(i >= 3)
        def _():
            pair_done(w.at[pl.ds(2 * b, 2), :, :, :, 1 - c], b).wait_recv()
            project(2 * b)
            local_state(2 * b, 2 * b)

        for k in (5, 3, 1):
            valid(k, i - k // 2)

        @pl.when(i == 4)
        def _():
            scan_step(2, 0)

        @pl.when(i >= 3)
        def _():
            project(2 * b + 1)
            local_state(2 * b + 1, 2 * b + 1)
            swap_copy(b).start()

        return 0

    lax.fori_loop(0, 5, slot, 0)
    weight_round(6, NB - 1)
    scan_step(3, 0)
    scan_step(1, 1)
    pair_done(w.at[pl.ds(NU - 2, 2), :, :, :, 1 - c], NB - 1).wait_recv()
    project(4)

    def gathered(h):
        hop(x_ring(h), 2)
        mix(h, h == 0, h == NH - 1)

    attention(4, 0, 0)
    scan_step(4, 0)
    normed(0)
    attention(4, 1, 1)
    normed(1)
    scan_step(2, 1)
    project(5)
    scan_step(3, 1)
    hop(x_ring(0), 1)
    attention(5, 0, 2)
    scan_step(4, 1)
    normed(2)
    hop(x_ring(1), 1)
    attention(5, 1, 3)
    normed(3)
    ow_load.wait()
    gathered(0)
    hop(x_ring(2), 1)
    gathered(1)
    hop(x_ring(3), 1)
    gathered(2)
    gathered(3)
    finish()

    def end(h, _):
        sent(nb.at[h, pl.ds(0, 3)], xs_sem.at[h])
        return 0

    lax.fori_loop(0, NH, end, 0)
    for q in range(2):
        swap_copy(q).wait_send()
        sent(tz.at[q, pl.ds(0, 7)], zs_sem.at[q])
        sent(ty.at[q, pl.ds(0, 3)], ys_sem.at[q])
        hand_copy(q, c).wait_send()


def fused(tokens, wq, wk, wv, ow, gate, rate, gain):
    rows, depth = tokens.shape
    any_spec = pl.BlockSpec(memory_space=pl.ANY)
    vmem = pl.BlockSpec(memory_space=pltpu.VMEM)
    bf16, f32, dma = jnp.bfloat16, jnp.float32, pltpu.SemaphoreType.DMA
    return pl.pallas_call(
        kernel,
        out_shape=jax.ShapeDtypeStruct((rows, ow.shape[-1]), bf16),
        in_specs=[any_spec] * 5 + [vmem, pl.BlockSpec(memory_space=pltpu.SMEM), vmem],
        out_specs=vmem,
        scratch_shapes=[
            pltpu.VMEM((rows, depth), bf16),
            pltpu.VMEM((NU, 2, NY, NZ, 2, 64, 128), bf16),
            pltpu.VMEM((NY, NZ, 2, 16, 128), bf16),
            pltpu.VMEM((128, depth), bf16),
            pltpu.VMEM(ow.shape, bf16),
            pltpu.VMEM((NU, rows, 256), bf16),
            pltpu.VMEM((NH, rows, 128), f32),
            pltpu.VMEM((NH, 8, rows), f32),
            pltpu.VMEM((NH, 8, 128), f32),
            pltpu.VMEM((NH, 128, 128), f32),
            pltpu.VMEM((2, 2, 2, 72, 128), f32),
            pltpu.VMEM((2, NZ, 2, 80, 128), bf16),
            pltpu.VMEM((2, NY, 2, 80, 128), bf16),
            pltpu.VMEM((2, 2, 64, 128), bf16),
            pltpu.VMEM((NH, 128, 128), bf16),
            pltpu.VMEM((NH, rows, 128), f32),
            pltpu.VMEM((NH, rows, 128), bf16),
            pltpu.VMEM((NH, NX, rows, 128), bf16),
            pltpu.VMEM((rows, ow.shape[-1]), f32),
            dma((2 * NU + 3,)), dma((NB, 76)), dma((NB, 4)), dma((12,)), dma((2,)),
            dma((NB + 1,)), dma((NB + 1,)),
            dma((2, 2)), dma((2,)), dma((2, 8)), dma((2,)), dma((2, 4)), dma((2, 2)),
            dma((NH,)), dma((NH, 4)),
        ],
        compiler_params=pltpu.CompilerParams(
            collective_id=0, has_side_effects=True, vmem_limit_bytes=63 * 1024 * 1024
        ),
    )(tokens, wq, wk, wv, ow, gate, rate, gain)


def on_device(tokens, wq, wk, wv, wg, decay_rate, norm_gain, out_weight):
    ow = out_weight.reshape(NX, NH, 128, out_weight.shape[1])
    return fused(tokens, wq, wk, wv, ow, wg, decay_rate, norm_gain.reshape(NH, 128))


def solution(mesh):
    return jax.shard_map(
        on_device,
        mesh=mesh,
        in_specs=(
            P("seq", None), P("seq", "tp"), P("seq", "tp"), P("seq", "tp"), P("seq", "tp"),
            P("tp"), P("tp"), P(None, "tp"),
        ),
        out_specs=P("seq", "tp"),
        check_vma=False,
    )
```

time: 138 us -> 112 us (0.81)
  Pallas kernels: 131 us -> 107 us
    pallas_call x1, Pallas kernels: 131 us -> 107 us  [fused(): pl.pallas_call(kernel, out_shape=jax.ShapeDtypeStruct((rows, ow.shape[-1]...]
    broadcast_in_dim x2 -> x0, local copies, waits for them, and re-layouts: 1.94 us -> none  [the longest x1 1.29 us: on_device(): gain = jnp.broadcast_to(norm_gain.reshape(NH, 1, 128), (NH, 8, 128))]
    unnamed x1 -> x2, local copies, waits for them, and re-layouts: 2.67 us -> 4.05 us
where the time goes in v3:
time: 112 us; the launch traced here: 111 us
  Pallas kernels  107 us (96%)
  local copies, waits for them, and re-layouts  4.05 us (4%)
    pallas_call x1, Pallas kernels, fused(): pl.pallas_call(kernel, out_shape=jax.ShapeDtypeStruct((rows, ow.shape[-1]...  107 us
    unnamed x2, local copies, waits for them, and re-layouts  4.05 us

profile of v3, /device:TPU:1, one launch (start us, length us, event | category | flops | bytes accessed | tf_op | source)
XLA Modules:
  0.0 111.5 jit_solution(5345887509831146662)
XLA Ops:
  0.0 1.4 %copy.9.gate_ref = bf16[64,4]{1,0:T(8,128)(2,1)} copy(bf16[64,4]{0,1:T(4,128)(2,1)} %param.12) | data formatting | bytes 1024 | tf_op args[4]
  1.4 107.4 %shard_map.82 = bf16[768,1024]{1,0:T(8,128)(2,1)} custom-call(bf16[768,4096]{1,0:T(8,128)(2,1)} %tok_hbm.1, bf16[64,512]{1,0:T(8,128)(2,1)} %wq_hbm.1, bf16[64,512]{1,0:T(8,128)(2,1)} %wk_hbm.1, bf16[64,512]{1,0:T(8,128)(2,1)} %wv_hbm.1, bf16[4,4,128,1024]{3,2,1,0:T(8,128)(2,1)} %bitcast.2, bf16[64,4]{1,0:T(8,128)(2,1)} %copy.9.gate_ref, f32[4]{0:T(128)} %rate_ref.1, ...), custom_call_target="tpu_custom_call" | custom-call | tf_op jit(solution)/shard_map/pallas_call | solution.py:524
  108.8 2.7 %copy.11 = bf16[768,1024]{1,0:T(8,128)(2,1)} copy(bf16[768,1024]{1,0:T(8,128)(2,1)} %shard_map.82) | data formatting | bytes 3145728

commit v4 on v3

--- a/solution.py
+++ b/solution.py
@@ -55,6 +55,33 @@
             ).wait_recv()
 
 
+class Direct:
+    n = 2
+
+    def __init__(self, item, pos, peers, recv, send):
+        self.item, self.pos, self.peers = item, pos, peers
+        self.recv_sem, self.send_sem = recv, send
+
+    def copy(self, idx, d):
+        ref = self.item(idx, None)
+        return pltpu.make_async_remote_copy(
+            src_ref=ref,
+            dst_ref=ref,
+            send_sem=self.send_sem,
+            recv_sem=self.recv_sem(d - 1),
+            device_id=self.peers[d - 1],
+            device_id_type=MESH,
+        )
+
+    def send(self, r):
+        for d in range(1, len(self.peers) + 1):
+            self.copy(self.pos, d).start()
+
+    def recv(self, r):
+        for d in range(1, len(self.peers) + 1):
+            self.copy(self.pos - d, d).wait_recv()
+
+
 def thirds(v):
     hi = v.astype(jnp.bfloat16).astype(jnp.float32)
     mid = (v - hi).astype(jnp.bfloat16).astype(jnp.float32)
@@ -79,6 +106,8 @@
     yp, ym = seq_id(y + 1, z, c), seq_id(y - 1, z, c)
     zp, zm = seq_id(y, z + 1, c), seq_id(y, z - 1, c)
     mate = seq_id(y, z, 1 - c)
+    y_peers = [seq_id(y + d, z, c) for d in range(1, NY)]
+    z_peers = [seq_id(y, z + d, c) for d in range(1, NZ)]
     xp, xm = {"tp": lax.rem(x + 1, NX)}, {"tp": lax.rem(x + NX - 1, NX)}
 
     loads = []
@@ -91,17 +120,15 @@
     for cp in loads:
         cp.start()
     tok_load = pltpu.make_async_copy(tok_hbm, tok, load_sem.at[2 * NU + 1])
-    tok_load.start()
     ow_load = pltpu.make_async_copy(ow_hbm, ow, load_sem.at[2 * NU + 2])
-    ow_load.start()
 
     barrier = pltpu.get_barrier_semaphore()
-    partners = [seq_id(y, z + d, c) for d in range(1, NZ)]
-    partners += [seq_id(y + d, z, c) for d in range(1, NY)]
-    partners += [mate, xp, xm]
+    partners = z_peers + y_peers + [mate, xp, xm]
     for dev in partners:
         pl.semaphore_signal(barrier, inc=1, device_id=dev, device_id_type=MESH)
     pl.semaphore_wait(barrier, len(partners))
+    tok_load.start()
+    ow_load.start()
 
     def rows(part):
         return slice(None) if part is None else pl.ds(part * 32, 32)
@@ -111,31 +138,34 @@
 
     def rings(b):
         made = []
-
-        def make(item, along_y, wait):
-            count = len(made)
-            base = (0, 4, 12, 20, 28, 36)[count] if count < 6 else 44 + 4 * (count - 6)
-            made.append((wait, Ring(
-                item, NY if along_y else NZ, y if along_y else z,
-                yp if along_y else zp, ym if along_y else zm,
-                lambda i: recv_sem.at[b, base + i], send_sem.at[b, count if count < 2 else 2 if count < 6 else 3],
-            )))
-
-        make(lambda i, p: piece(b, 0, i, z, p), True, 0)
-        make(lambda i, p: piece(b, 1, y, i, p), False, 0)
+        base = 0
+
+        def make(item, along_y, wait, k):
+            nonlocal base
+            first = base
+            recv, send = lambda i: recv_sem.at[b, first + i], send_sem.at[b, k]
+            if along_y:
+                ring = Direct(item, y, y_peers, recv, send)
+                base += NY - 1
+            else:
+                ring = Ring(item, NZ, z, zp, zm, recv, send)
+                base += NZ
+            made.append((wait, ring))
+
+        make(lambda i, p: piece(b, 0, i, z, p), True, 0, 0)
+        make(lambda i, p: piece(b, 1, y, i, p), False, 0, 1)
         for d in (0, 1, -1, 2):
-            make(lambda i, p, d=d: piece(b, 0, y + d, i, p), False, abs(d))
+            make(lambda i, p, d=d: piece(b, 0, y + d, i, p), False, min(abs(d), 1), 2)
         for d in (0, 1, -1, 2, -2, 3, -3, 4):
-            make(lambda i, p, d=d: piece(b, 1, i, z + d, p), True, abs(d))
+            make(lambda i, p, d=d: piece(b, 1, i, z + d, p), True, abs(d), 3)
         return made
 
-    g1 = Ring(lambda i, p: gb.at[i, z, c], NY, y, yp, ym,
-              lambda i: grecv_sem.at[i], gsend_sem.at[0], split=False)
-    g2 = Ring(lambda i, p: gb.at[:, i, c], NZ, z, zp, zm,
-              lambda i: grecv_sem.at[4 + i], gsend_sem.at[1], split=False)
-
-    def to_mate(ring, idx, k):
-        ref = ring.item(lax.rem(idx + 2 * ring.n, ring.n), None)
+    g1 = Direct(lambda i, p: gb.at[lax.rem(i + NY, NY), z, c], y, y_peers,
+                lambda i: grecv_sem.at[i], gsend_sem.at[0])
+    g2 = Direct(lambda i, p: gb.at[:, lax.rem(i + NZ, NZ), c], z, z_peers,
+                lambda i: grecv_sem.at[4 + i], gsend_sem.at[1])
+
+    def to_mate(ref, k):
         pltpu.make_async_remote_copy(
             src_ref=ref, dst_ref=ref, send_sem=pair_send.at[k], recv_sem=pair_recv.at[k],
             device_id=mate, device_id_type=MESH,
@@ -152,27 +182,26 @@
         lane = lax.broadcasted_iota(jnp.int32, (64, 128), 1)
         pick = jnp.where(lane == k + 64 * c, 1.0, 0.0).astype(jnp.bfloat16)
         turned = lax.dot_general(
-            gate_ref[...], pick, (((0,), (0,)), ((), ())), preferred_element_type=jnp.float32
+            gate_ref[...], pick, (((1,), (0,)), ((), ())), preferred_element_type=jnp.float32
         )
         gb[y, z, c] = jnp.concatenate(
             [turned, jnp.zeros((12, 128), jnp.float32)], axis=0
         ).astype(jnp.bfloat16)
 
     def column(b, zz):
-        ref = w.at[pl.ds(2 * b, 2), :, :, lax.rem(zz + NZ, NZ), c]
-        pltpu.make_async_remote_copy(
-            src_ref=ref, dst_ref=ref, send_sem=pair_send.at[b], recv_sem=pair_recv.at[b],
-            device_id=mate, device_id_type=MESH,
-        ).start()
+        to_mate(w.at[pl.ds(2 * b, 2), :, :, lax.rem(zz + NZ, NZ), c], b)
 
     def gate_round(k):
-        if k <= 2:
-            hop(g1, k)
-        if k >= 2:
-            hop(g2, k - 2)
-            d = k - 2
-            for at in {0: (z,), 4: (z + 4,)}.get(d, (z + d, z - d)):
-                to_mate(g2, at, NB)
+        if k == 0:
+            g1.send(0)
+        elif k == 1:
+            g1.recv(0)
+            g2.send(0)
+            to_mate(g2.item(z, None), NB)
+        else:
+            g2.recv(0)
+            for d in range(1, NZ):
+                to_mate(g2.item(z - d, None), NB)
 
     def weight_round(k, b):
         if k == 0:
@@ -181,29 +210,16 @@
                     own = w.at[2 * b + i, t, y, z, c]
                     pltpu.make_async_copy(own, own, load_sem.at[b * 4 + 2 * i + t]).wait()
 
-            @pl.when(b == 0)
-            def _():
-                load_gate()
-
-        @pl.when(b == 0)
-        def _():
-            gate_round(k)
-
         todo = [(ring, k - wait) for wait, ring in rings(b)]
         for ring, r in todo:
             if 0 < r <= ring.n // 2:
                 ring.recv(r - 1)
             if 0 <= r < ring.n // 2:
                 ring.send(r)
-        if k >= 2:
-            d = k - 2
+        if k >= 1:
+            d = k - 1
             for at in {0: (z,), 4: (z + 4,)}.get(d, (z + d, z - d)):
                 column(b, at)
-
-    def valid(k, b):
-        @pl.when((b >= 0) & (b < NB))
-        def _():
-            weight_round(k, b)
 
     def pair_done(ref, k):
         return pltpu.make_async_remote_copy(
@@ -433,53 +449,54 @@
 
         lax.fori_loop(0, 3, chunk, 0)
 
-    def slot(i, _):
-        b = i - 3
-        for k in (6, 4, 2, 0):
-            valid(k, i - k // 2)
-
-        @pl.when(i == 3)
+    def arrived(b):
+        pair_done(w.at[pl.ds(2 * b, 2), :, :, :, 1 - c], b).wait_recv()
+
+    def key_value(u):
+        project(u)
+        local_state(u, u)
+
+    def slot(t, _):
+        for k in range(5, -1, -1):
+            @pl.when((t >= k) & (t < k + NB))
+            def _():
+                weight_round(k, t - k)
+
+        for k in range(3):
+            pl.when(t == k)(lambda k=k: gate_round(k))
+
+        @pl.when(t == 3)
         def _():
             pair_done(gb.at[:, :, 1 - c], NB).wait_recv()
             tok_load.wait()
             gate()
 
-        @pl.when(i == 4)
+        @pl.when(t == 6)
         def _():
             scan_step(1, 0)
 
-        @pl.when(i >= 3)
+        @pl.when(t >= 5)
         def _():
-            pair_done(w.at[pl.ds(2 * b, 2), :, :, :, 1 - c], b).wait_recv()
-            project(2 * b)
-            local_state(2 * b, 2 * b)
-
-        for k in (5, 3, 1):
-            valid(k, i - k // 2)
-
-        @pl.when(i == 4)
-        def _():
-            scan_step(2, 0)
-
-        @pl.when(i >= 3)
-        def _():
-            project(2 * b + 1)
-            local_state(2 * b + 1, 2 * b + 1)
+            b = t - 5
+            arrived(b)
+            key_value(2 * b)
+            key_value(2 * b + 1)
             swap_copy(b).start()
 
         return 0
-
-    lax.fori_loop(0, 5, slot, 0)
-    weight_round(6, NB - 1)
-    scan_step(3, 0)
-    scan_step(1, 1)
-    pair_done(w.at[pl.ds(NU - 2, 2), :, :, :, 1 - c], NB - 1).wait_recv()
-    project(4)
 
     def gathered(h):
         hop(x_ring(h), 2)
         mix(h, h == 0, h == NH - 1)
 
+    load_gate()
+    lax.fori_loop(0, 7, slot, 0)
+    weight_round(5, NB - 1)
+    scan_step(2, 0)
+    scan_step(1, 1)
+    arrived(2)
+    project(4)
+    scan_step(3, 0)
     attention(4, 0, 0)
     scan_step(4, 0)
     normed(0)
@@ -546,7 +563,7 @@
             pltpu.VMEM((NH, rows, 128), bf16),
             pltpu.VMEM((NH, NX, rows, 128), bf16),
             pltpu.VMEM((rows, ow.shape[-1]), f32),
-            dma((2 * NU + 3,)), dma((NB, 76)), dma((NB, 4)), dma((12,)), dma((2,)),
+            dma((2 * NU + 3,)), dma((NB, 67)), dma((NB, 4)), dma((12,)), dma((2,)),
             dma((NB + 1,)), dma((NB + 1,)),
             dma((2, 2)), dma((2,)), dma((2, 8)), dma((2,)), dma((2, 4)), dma((2, 2)),
             dma((NH,)), dma((NH, 4)),
@@ -559,7 +576,7 @@
 
 def on_device(tokens, wq, wk, wv, wg, decay_rate, norm_gain, out_weight):
     ow = out_weight.reshape(NX, NH, 128, out_weight.shape[1])
-    return fused(tokens, wq, wk, wv, ow, wg, decay_rate, norm_gain.reshape(NH, 128))
+    return fused(tokens, wq, wk, wv, ow, wg.T, decay_rate, norm_gain.reshape(NH, 128))
 
 
 def solution(mesh):

time: 112 us -> 109 us (0.973)
  local copies, waits for them, and re-layouts: 4.05 us -> 2.67 us
    pallas_call x1, Pallas kernels: 107 us -> 106 us  [fused(): pl.pallas_call(kernel, out_shape=jax.ShapeDtypeStruct((rows, ow.shape[-1]...]
    unnamed x2 -> x1, local copies, waits for them, and re-layouts: 4.05 us -> 2.67 us
where the time goes in v4:
time: 109 us
  Pallas kernels  106 us (97%)
  local copies, waits for them, and re-layouts  2.67 us (2%)
    pallas_call x1, Pallas kernels, fused(): pl.pallas_call(kernel, out_shape=jax.ShapeDtypeStruct((rows, ow.shape[-1]...  106 us
    unnamed x1, local copies, waits for them, and re-layouts  2.67 us

profile of v4, /device:TPU:1, one launch (start us, length us, event | category | flops | bytes accessed | tf_op | source)
XLA Modules:
  0.0 108.6 jit_solution(2000743358843395316)
XLA Ops:
  0.0 105.9 %shard_map.82 = bf16[768,1024]{1,0:T(8,128)(2,1)} custom-call(bf16[768,4096]{1,0:T(8,128)(2,1)} %tok_hbm.1, bf16[64,512]{1,0:T(8,128)(2,1)} %wq_hbm.1, bf16[64,512]{1,0:T(8,128)(2,1)} %wk_hbm.1, bf16[64,512]{1,0:T(8,128)(2,1)} %wv_hbm.1, bf16[4,4,128,1024]{3,2,1,0:T(8,128)(2,1)} %bitcast.3, bf16[4,64]{1,0:T(4,128)(2,1)} %bitcast.5, f32[4]{0:T(128)} %rate_ref.1, ...), custom_call_target="tpu_custom_call" | custom-call | tf_op jit(solution)/shard_map/pallas_call | solution.py:541
  105.9 2.7 %copy.10 = bf16[768,1024]{1,0:T(8,128)(2,1)} copy(bf16[768,1024]{1,0:T(8,128)(2,1)} %shard_map.82) | data formatting | bytes 3145728

commit v5 on v4

--- a/solution.py
+++ b/solution.py
@@ -491,12 +491,12 @@
 
     load_gate()
     lax.fori_loop(0, 7, slot, 0)
-    weight_round(5, NB - 1)
     scan_step(2, 0)
     scan_step(1, 1)
+    weight_round(5, NB - 1)
+    scan_step(3, 0)
     arrived(2)
     project(4)
-    scan_step(3, 0)
     attention(4, 0, 0)
     scan_step(4, 0)
     normed(0)

time: 109 us -> 110 us (level); the launches traced: 109 us -> 108 us
  no operation moved by 1% of the time
where the time goes in v5:
time: 110 us; the launch traced here: 108 us
  Pallas kernels  106 us (96%)
  local copies, waits for them, and re-layouts  2.67 us (2%)
    pallas_call x1, Pallas kernels, fused(): pl.pallas_call(kernel, out_shape=jax.ShapeDtypeStruct((rows, ow.shape[-1]...  106 us
    unnamed x1, local copies, waits for them, and re-layouts  2.67 us

profile of v5, /device:TPU:1, one launch (start us, length us, event | category | flops | bytes accessed | tf_op | source)
XLA Modules:
  0.0 108.2 jit_solution(2999804298081588211)
XLA Ops:
  0.0 105.5 %shard_map.82 = bf16[768,1024]{1,0:T(8,128)(2,1)} custom-call(bf16[768,4096]{1,0:T(8,128)(2,1)} %tok_hbm.1, bf16[64,512]{1,0:T(8,128)(2,1)} %wq_hbm.1, bf16[64,512]{1,0:T(8,128)(2,1)} %wk_hbm.1, bf16[64,512]{1,0:T(8,128)(2,1)} %wv_hbm.1, bf16[4,4,128,1024]{3,2,1,0:T(8,128)(2,1)} %bitcast.3, bf16[4,64]{1,0:T(4,128)(2,1)} %bitcast.5, f32[4]{0:T(128)} %rate_ref.1, ...), custom_call_target="tpu_custom_call" | custom-call | tf_op jit(solution)/shard_map/pallas_call | solution.py:541
  105.5 2.7 %copy.10 = bf16[768,1024]{1,0:T(8,128)(2,1)} copy(bf16[768,1024]{1,0:T(8,128)(2,1)} %shard_map.82) | data formatting | bytes 3145728

commit v6 on v4

--- a/solution.py
+++ b/solution.py
@@ -496,17 +496,17 @@
     scan_step(1, 1)
     arrived(2)
     project(4)
+    attention(4, 0, 0)
     scan_step(3, 0)
-    attention(4, 0, 0)
+    attention(4, 1, 1)
     scan_step(4, 0)
     normed(0)
-    attention(4, 1, 1)
     normed(1)
     scan_step(2, 1)
     project(5)
+    attention(5, 0, 2)
     scan_step(3, 1)
     hop(x_ring(0), 1)
-    attention(5, 0, 2)
     scan_step(4, 1)
     normed(2)
     hop(x_ring(1), 1)

time: 109 us -> 109 us (level)
  no operation moved by 1% of the time
where the time goes in v6:
time: 109 us
  Pallas kernels  106 us (97%)
  local copies, waits for them, and re-layouts  2.67 us (2%)
    pallas_call x1, Pallas kernels, fused(): pl.pallas_call(kernel, out_shape=jax.ShapeDtypeStruct((rows, ow.shape[-1]...  106 us
    unnamed x1, local copies, waits for them, and re-layouts  2.67 us

profile of v6, /device:TPU:1, one launch (start us, length us, event | category | flops | bytes accessed | tf_op | source)
XLA Modules:
  0.0 108.6 jit_solution(12234574339700507136)
XLA Ops:
  0.0 105.9 %shard_map.82 = bf16[768,1024]{1,0:T(8,128)(2,1)} custom-call(bf16[768,4096]{1,0:T(8,128)(2,1)} %tok_hbm.1, bf16[64,512]{1,0:T(8,128)(2,1)} %wq_hbm.1, bf16[64,512]{1,0:T(8,128)(2,1)} %wk_hbm.1, bf16[64,512]{1,0:T(8,128)(2,1)} %wv_hbm.1, bf16[4,4,128,1024]{3,2,1,0:T(8,128)(2,1)} %bitcast.3, bf16[4,64]{1,0:T(4,128)(2,1)} %bitcast.5, f32[4]{0:T(128)} %rate_ref.1, ...), custom_call_target="tpu_custom_call" | custom-call | tf_op jit(solution)/shard_map/pallas_call | solution.py:541
  105.9 2.7 %copy.10 = bf16[768,1024]{1,0:T(8,128)(2,1)} copy(bf16[768,1024]{1,0:T(8,128)(2,1)} %shard_map.82) | data formatting | bytes 3145728
